TPU v7x, 32 devices: a whole 2x2x4 slice. The times are simulated.
32 devices in a mesh: gx: 4 (over z), gy: 2 (over x), gz: 4 (over y, core).
Axes of the slice: x: 2, y: 2, z: 4, core: 2. Of those that a mesh axis runs over, the one named last changes fastest.
Arguments:
- displacement: float32 [3, 32, 32, 512], P(None, 'gx', 'gy', 'gz'), may hold values from -100 to 100
- density: float32 [32, 32, 512], P('gx', 'gy', 'gz'), may hold values from 0.1 to 1
Outputs:
- aggregate: float32 [], replicated
- adjoint: float32 [3, 32, 32, 512], P(None, 'gx', 'gy', 'gz')
- sensitivity: float32 [32, 32, 512], P('gx', 'gy', 'gz')
All inputs are finite; a program needn't handle non-finite values.
Results may differ from a plain program's by a relative error of at most 0.0003.
Values sent between devices are 32-bit elements; how exact they have to be, the bound alone decides.
A program may use at most 64 MiB of HBM per device.

v0:
```python
import math

import jax
import jax.numpy as jnp
from jax import lax
from jax.sharding import PartitionSpec as P

ITERS = 6


lame_first = 0.3 / (1.3 * 0.4)
shear_modulus = 1.0 / 2.6
power_scale = 3.0
damping = 0.6
shift_term = 0.1
diag_factor = (lame_first + 3.0 * shear_modulus) / 16.0
CORNERS = [(first, second, third) for first in (0, 1) for second in (0, 1) for third in (0, 1)]
OFFSETS = [
    ((first, second, third), 2.5 - math.sqrt(first * first + second * second + third * third))
    for first in range(-2, 3)
    for second in range(-2, 3)
    for third in range(-2, 3)
    if first * first + second * second + third * third <= 4
]


def passed_along(block, axis, distance):
    devices = range(lax.axis_size(axis))
    route = [(i - distance, i) for i in devices if i - distance in devices]
    return lax.ppermute(block, axis, route)


def extended(array, sides, width):
    for axis, dim in sides:
        count, length = (lax.axis_size(axis), array.shape[dim])
        up = [(i, (i + 1) % count) for i in range(count - 1)]
        down = [(j, i) for i, j in up]
        last = lax.slice_in_dim(array, length - width, length, axis=dim)
        leading = lax.slice_in_dim(array, 0, width, axis=dim)
        before = lax.ppermute(last, axis, up)
        after = lax.ppermute(leading, axis, down)
        array = jnp.concatenate([before, array, after], axis=dim)
    return array


def window(array, anchor, extent):
    return array[
        :,
        anchor[0] : anchor[0] + extent[0],
        anchor[1] : anchor[1] + extent[1],
        anchor[2] : anchor[2] + extent[2],
    ]


def window_cells(array, anchor, extent):
    return array[
        anchor[0] : anchor[0] + extent[0],
        anchor[1] : anchor[1] + extent[1],
        anchor[2] : anchor[2] + extent[2],
    ]


def gradients(padded, offset, extent):
    totals = [0.0, 0.0, 0.0]
    for corner in CORNERS:
        piece = window(padded, (offset + corner[0], offset + corner[1], offset + corner[2]), extent)
        for direction in range(3):
            totals[direction] = totals[direction] + (2 * corner[direction] - 1) * piece
    return 0.25 * jnp.concatenate(totals, axis=0)


def strains(grad_all):
    return [
        grad_all[0],
        grad_all[4],
        grad_all[8],
        grad_all[3] + grad_all[1],
        grad_all[7] + grad_all[5],
        grad_all[2] + grad_all[6],
    ]


def stiffen(values):
    trace = values[0] + values[1] + values[2]
    return [
        lame_first * trace + 2.0 * shear_modulus * values[0],
        lame_first * trace + 2.0 * shear_modulus * values[1],
        lame_first * trace + 2.0 * shear_modulus * values[2],
        shear_modulus * values[3],
        shear_modulus * values[4],
        shear_modulus * values[5],
    ]


def spread(terms):
    return jnp.stack(
        [terms[0], terms[3], terms[5], terms[3], terms[1], terms[4], terms[5], terms[4], terms[2]],
        axis=0,
    )


def assemble(padded, extent):
    result = 0.0
    for corner in CORNERS:
        anchor = (1 - corner[0], 1 - corner[1], 1 - corner[2])
        for direction in range(3):
            piece = window(padded[3 * direction : 3 * direction + 3], anchor, extent)
            result = result + 0.25 * (2 * corner[direction] - 1) * piece
    return result


def mises(sigma):
    return (
        sigma[0] * sigma[0]
        + sigma[1] * sigma[1]
        + sigma[2] * sigma[2]
        - sigma[0] * sigma[1]
        - sigma[1] * sigma[2]
        - sigma[2] * sigma[0]
        + 3.0 * (sigma[3] * sigma[3] + sigma[4] * sigma[4] + sigma[5] * sigma[5])
    )


def mises_slope(sigma):
    return [
        2.0 * sigma[0] - sigma[1] - sigma[2],
        2.0 * sigma[1] - sigma[2] - sigma[0],
        2.0 * sigma[2] - sigma[0] - sigma[1],
        6.0 * sigma[3],
        6.0 * sigma[4],
        6.0 * sigma[5],
    ]


def nodes_above(field):
    received = passed_along(field[:, :1], "gx", -1)
    field = jnp.concatenate([field, received], axis=1)
    received = passed_along(field[:, :, :1], "gy", -1)
    field = jnp.concatenate([field, received], axis=2)
    received = passed_along(field[:, :, :, :1], "gz", -1)
    return jnp.concatenate([field, received], axis=3)


def terms_below(terms):
    received = passed_along(terms[:, -1:], "gx", 1)
    terms = jnp.concatenate([received, terms], axis=1)
    received = passed_along(terms[:, :, -1:], "gy", 1)
    terms = jnp.concatenate([received, terms], axis=2)
    received = passed_along(terms[:, :, :, -1:], "gz", 1)
    return jnp.concatenate([received, terms], axis=3)


def dens_below(values):
    received = passed_along(values[-1:], "gx", 1)
    values = jnp.concatenate([received, values], axis=0)
    received = passed_along(values[:, -1:], "gy", 1)
    values = jnp.concatenate([received, values], axis=1)
    received = passed_along(values[:, :, -1:], "gz", 1)
    return jnp.concatenate([received, values], axis=2)


def node_rim_deep(field):
    return extended(field, (("gx", 1), ("gy", 2), ("gz", 3)), 1)


def inside_line(position, count, length, lower, upper):
    cell_index = position * length + jnp.arange(-lower, length + upper, dtype=jnp.int32)
    limit = count * length
    return ((cell_index >= 0) & (cell_index < limit)).astype(jnp.float32)


def inside_block(extent, lower, upper):
    counts = (lax.axis_size("gx"), lax.axis_size("gy"), lax.axis_size("gz"))
    first = inside_line(lax.axis_index("gx"), counts[0], extent[0], lower, upper)
    second = inside_line(lax.axis_index("gy"), counts[1], extent[1], lower, upper)
    third = inside_line(lax.axis_index("gz"), counts[2], extent[2], lower, upper)
    return first[:, None, None] * second[None, :, None] * third[None, None, :]


def on_device(displacement, density):
    extent = density.shape
    widened = (extent[0] + 1, extent[1] + 1, extent[2] + 1)
    elements = (
        extent[0]
        * extent[1]
        * extent[2]
        * lax.axis_size("gx")
        * lax.axis_size("gy")
        * lax.axis_size("gz")
    )
    inside_low = inside_block(extent, 1, 0)
    inside = inside_block(extent, 2, 2)
    lowered = dens_below(density)
    stiff_low = (0.01 + 0.99 * lowered**3) * inside_low
    base = stiffen(strains(gradients(nodes_above(displacement), 0, extent)))
    rooted = jnp.sqrt(density)
    sigma = [rooted * value for value in base]
    stress = jnp.sqrt(mises(sigma) + 1.0)
    score = power_scale * stress
    local_top = jnp.max(score)
    top = lax.pmax(local_top, ("gx", "gy", "gz"))
    total = lax.psum(jnp.sum(jnp.exp(score - top)), ("gx", "gy", "gz"))
    aggregate = (top + jnp.log(total)) / power_scale
    weight = jnp.exp(score - top) / total * float(elements)
    factor = weight / (2.0 * stress)
    slope = [factor * value for value in mises_slope(sigma)]
    load = assemble(terms_below(spread(stiffen([rooted * value for value in slope]))), extent)
    summed = 0.0
    for corner in CORNERS:
        summed = summed + window_cells(
            stiff_low, (1 - corner[0], 1 - corner[1], 1 - corner[2]), extent
        )
    diag = diag_factor * summed + shift_term

    def operate(field):
        values = stiffen(strains(gradients(node_rim_deep(field), 0, widened)))
        forces = assemble(spread([stiff_low * value for value in values]), extent)
        return forces + shift_term * field

    adjoint = damping * load / diag
    for sweep in range(1, ITERS):
        adjoint = adjoint + damping * (load - operate(adjoint)) / diag
    other = strains(gradients(nodes_above(adjoint), 0, extent))
    explicit = sum((slope[index] * base[index] for index in range(6))) / (2.0 * rooted)
    worked = sum((base[index] * other[index] for index in range(6)))
    raw = explicit - 2.97 * density * density * worked
    hsum = 0.0
    for offset, factor_w in OFFSETS:
        hsum = hsum + factor_w * window_cells(
            inside, (2 + offset[0], 2 + offset[1], 2 + offset[2]), extent
        )
    scaled = extended(raw / hsum, (("gx", 0), ("gy", 1), ("gz", 2)), 2)
    sensitivity = 0.0
    for offset, factor_w in OFFSETS:
        sensitivity = sensitivity + factor_w * window_cells(
            scaled, (2 + offset[0], 2 + offset[1], 2 + offset[2]), extent
        )
    return (aggregate, adjoint, sensitivity)


def solution(mesh):
    return jax.shard_map(
        on_device,
        mesh=mesh,
        in_specs=(P(None, "gx", "gy", "gz"), P("gx", "gy", "gz")),
        out_specs=(P(), P(None, "gx", "gy", "gz"), P("gx", "gy", "gz")),
        check_vma=False,
    )
```

profile of v0, /device:TPU:1, one launch (start us, length us, event | category | flops | bytes accessed | tf_op | source)
XLA Modules:
  0.0 356.6 jit_solution(12985279084028826532)
XLA Ops:
  3.4 4.6 %collective-permute-start.6 = (f32[1,16,128]{2,1,0:T(8,128)S(1)}, f32[1,16,128]{2,1,0:T(8,128)S(1)}, u32[]{:S(2)}, u32[]{:S(2)}) collective-permute-start(f32[1,16,128]{2,1,0:T(8,128)S(1)} %slice.1477), channel_id=1, source_target_pairs={{0,8},{8,16},{16,24},{1,9},{9,17},{17,25},{2,10},{10,18},{18,26},{... | collective-permute-start | bytes 24584 | tf_op jit(solution)/shard_map/ppermute | solution.py:30
  10.5 3.1 collective-permute-done.1
  13.6 4.0 %collective-permute-start.2 = (f32[3,9,17,1]{3,2,1,0:T(8,128)S(1)}, f32[3,9,17,1]{3,2,1,0:T(8,128)S(1)}, u32[]{:S(2)}, u32[]{:S(2)}) collective-permute-start(f32[3,9,17,1]{3,2,1,0:T(8,128)S(1)} %fusion), channel_id=1, source_target_pairs={{1,0},{2,1},{3,2},{5,4},{6,5},{7,6},{9,8},{10,9},{11,10},{13,12},{... | collective-permute-start | bytes 5516 | tf_op jit(solution)/shard_map/ppermute | solution.py:30
  17.6 6.3 %collective-permute-done.2 = f32[3,9,17,1]{3,2,1,0:T(8,128)S(1)} collective-permute-done((f32[3,9,17,1]{3,2,1,0:T(8,128)S(1)}, f32[3,9,17,1]{3,2,1,0:T(8,128)S(1)}, u32[]{:S(2)}, u32[]{:S(2)}) %collective-permute-start.2) | collective-permute-done | bytes 1868 | tf_op jit(solution)/shard_map/ppermute | solution.py:30
  25.6 37.0 %pmax.7 = f32[]{:T(128)} all-reduce(f32[]{:T(128)} %get-tuple-element.34), channel_id=1, replica_groups=mesh['gx'=4,'gy'=2,'gz'=4] {'gx','gy','gz'}, use_global_device_ids=true, to_apply=%region_1.0 | all-reduce | flops 1 | bytes 8 | tf_op jit(solution)/shard_map/pmax | solution.py:201
  63.9 40.4 %psum.7 = f32[]{:T(128)} all-reduce(f32[]{:T(128)} %fusion.291), channel_id=1, replica_groups=mesh['gx'=4,'gy'=2,'gz'=4] {'gx','gy','gz'}, use_global_device_ids=true, to_apply=%region_3.0 | all-reduce | flops 1 | bytes 8 | tf_op jit(solution)/shard_map/psum | solution.py:202
  104.4 1.9 constant_dynamic-update-slice_fusion.10
  110.8 2.6 collective-permute-start.7
  114.1 3.4 collective-permute-start.3
  117.6 5.0 %collective-permute-start.8 = (f32[9,17,1]{2,1,0:T(8,128)S(1)}, f32[9,17,1]{2,1,0:T(8,128)S(1)}, u32[]{:S(2)}, u32[]{:S(2)}) collective-permute-start(f32[9,17,1]{2,1,0:T(8,128)S(1)} %fusion.185), channel_id=1, source_target_pairs={{0,1},{1,2},{2,3},{4,5},{5,6},{6,7},{8,9},{9,10},{10,11},{12,13},{... | collective-permute-start | bytes 1844 | tf_op jit(solution)/shard_map/ppermute | solution.py:30
  126.3 4.3 %collective-permute-start.5 = (f32[9,9,17,1]{2,3,1,0:T(1,128)S(1)}, f32[9,9,17,1]{2,3,1,0:T(1,128)S(1)}, u32[]{:S(2)}, u32[]{:S(2)}) collective-permute-start(f32[9,9,17,1]{2,3,1,0:T(1,128)S(1)} %copy.434), channel_id=1, source_target_pairs={{0,1},{1,2},{2,3},{4,5},{5,6},{6,7},{8,9},{9,10},{10,11},{12,13},{... | collective-permute-start | bytes 16532 | tf_op jit(solution)/shard_map/ppermute | solution.py:30
  130.6 1.6 fusion.275
  135.1 1.4 collective-permute-start.10
  136.5 4.0 %collective-permute-start.9 = (f32[3,1,16,128]{3,2,1,0:T(8,128)S(1)}, f32[3,1,16,128]{3,2,1,0:T(8,128)S(1)}, u32[]{:S(2)}, u32[]{:S(2)}) collective-permute-start(f32[3,1,16,128]{3,2,1,0:T(8,128)S(1)} %get-tuple-element.246), channel_id=1, source_target_pairs={{0,8},{8,16},{16,24},{1,9},{9,17},{17,25},{2,10},{10,18},{18,26},{... | collective-permute-start | bytes 73736 | tf_op jit(solution)/shard_map/ppermute | solution.py:40
  141.5 2.5 collective-permute-start.11
  145.3 3.2 collective-permute-done.12
  148.7 6.0 %collective-permute-start.13 = (f32[3,10,18,1]{3,2,1,0:T(8,128)S(1)}, f32[3,10,18,1]{3,2,1,0:T(8,128)S(1)}, u32[]{:S(2)}, u32[]{:S(2)}) collective-permute-start(f32[3,10,18,1]{3,2,1,0:T(8,128)S(1)} %get-tuple-element.216), channel_id=1, source_target_pairs={{0,1},{1,2},{2,3},{4,5},{5,6},{6,7},{8,9},{9,10},{10,11},{12,13},{... | collective-permute-start | bytes 6488 | tf_op jit(solution)/shard_map/ppermute | solution.py:40
  154.6 2.4 collective-permute-start.14
  157.6 1.5 collective-permute-done.13
  159.1 4.4 %collective-permute-done.14 = f32[3,10,18,1]{3,2,1,0:T(8,128)S(1)} collective-permute-done((f32[3,10,18,1]{3,2,1,0:T(8,128)S(1)}, f32[3,10,18,1]{3,2,1,0:T(8,128)S(1)}, u32[]{:S(2)}, u32[]{:S(2)}) %collective-permute-start.14) | collective-permute-done | bytes 2192 | tf_op jit(solution)/shard_map/ppermute | solution.py:41
  169.5 1.4 fusion.309
  171.3 3.9 %collective-permute-start.15 = (f32[3,1,16,128]{3,2,1,0:T(8,128)S(1)}, f32[3,1,16,128]{3,2,1,0:T(8,128)S(1)}, u32[]{:S(2)}, u32[]{:S(2)}) collective-permute-start(f32[3,1,16,128]{3,2,1,0:T(8,128)S(1)} %get-tuple-element.244), channel_id=1, source_target_pairs={{0,8},{8,16},{16,24},{1,9},{9,17},{17,25},{2,10},{10,18},{18,26},{... | collective-permute-start | bytes 73736 | tf_op jit(solution)/shard_map/ppermute | solution.py:40
  176.5 3.5 collective-permute-done.16
  180.1 1.4 collective-permute-start.17
  182.8 3.2 collective-permute-done.18
  186.2 4.3 %collective-permute-start.19 = (f32[3,10,18,1]{3,2,1,0:T(8,128)S(1)}, f32[3,10,18,1]{3,2,1,0:T(8,128)S(1)}, u32[]{:S(2)}, u32[]{:S(2)}) collective-permute-start(f32[3,10,18,1]{3,2,1,0:T(8,128)S(1)} %get-tuple-element.214), channel_id=1, source_target_pairs={{0,1},{1,2},{2,3},{4,5},{5,6},{6,7},{8,9},{9,10},{10,11},{12,13},{... | collective-permute-start | bytes 6488 | tf_op jit(solution)/shard_map/ppermute | solution.py:40
  190.5 2.1 collective-permute-start.20
  192.6 2.3 collective-permute-done.19
  194.9 4.4 %collective-permute-done.20 = f32[3,10,18,1]{3,2,1,0:T(8,128)S(1)} collective-permute-done((f32[3,10,18,1]{3,2,1,0:T(8,128)S(1)}, f32[3,10,18,1]{3,2,1,0:T(8,128)S(1)}, u32[]{:S(2)}, u32[]{:S(2)}) %collective-permute-start.20) | collective-permute-done | bytes 2192 | tf_op jit(solution)/shard_map/ppermute | solution.py:41
  206.8 3.6 %collective-permute-start.21 = (f32[3,1,16,128]{3,2,1,0:T(8,128)S(1)}, f32[3,1,16,128]{3,2,1,0:T(8,128)S(1)}, u32[]{:S(2)}, u32[]{:S(2)}) collective-permute-start(f32[3,1,16,128]{3,2,1,0:T(8,128)S(1)} %get-tuple-element.242), channel_id=1, source_target_pairs={{0,8},{8,16},{16,24},{1,9},{9,17},{17,25},{2,10},{10,18},{18,26},{... | collective-permute-start | bytes 73736 | tf_op jit(solution)/shard_map/ppermute | solution.py:40
  211.8 3.3 collective-permute-done.22
  215.0 1.4 collective-permute-start.23
  217.7 3.2 collective-permute-done.24
  221.1 4.6 %collective-permute-start.25 = (f32[3,10,18,1]{3,2,1,0:T(8,128)S(1)}, f32[3,10,18,1]{3,2,1,0:T(8,128)S(1)}, u32[]{:S(2)}, u32[]{:S(2)}) collective-permute-start(f32[3,10,18,1]{3,2,1,0:T(8,128)S(1)} %get-tuple-element.212), channel_id=1, source_target_pairs={{0,1},{1,2},{2,3},{4,5},{5,6},{6,7},{8,9},{9,10},{10,11},{12,13},{... | collective-permute-start | bytes 6488 | tf_op jit(solution)/shard_map/ppermute | solution.py:40
  225.7 2.1 collective-permute-start.26
  227.9 2.3 collective-permute-done.25
  230.2 4.4 %collective-permute-done.26 = f32[3,10,18,1]{3,2,1,0:T(8,128)S(1)} collective-permute-done((f32[3,10,18,1]{3,2,1,0:T(8,128)S(1)}, f32[3,10,18,1]{3,2,1,0:T(8,128)S(1)}, u32[]{:S(2)}, u32[]{:S(2)}) %collective-permute-start.26) | collective-permute-done | bytes 2192 | tf_op jit(solution)/shard_map/ppermute | solution.py:41
  242.0 3.0 collective-permute-start.27
  246.4 3.3 collective-permute-done.28
  249.6 1.4 collective-permute-start.29
  252.3 3.2 collective-permute-done.30
  255.7 4.6 %collective-permute-start.31 = (f32[3,10,18,1]{3,2,1,0:T(8,128)S(1)}, f32[3,10,18,1]{3,2,1,0:T(8,128)S(1)}, u32[]{:S(2)}, u32[]{:S(2)}) collective-permute-start(f32[3,10,18,1]{3,2,1,0:T(8,128)S(1)} %get-tuple-element.210), channel_id=1, source_target_pairs={{0,1},{1,2},{2,3},{4,5},{5,6},{6,7},{8,9},{9,10},{10,11},{12,13},{... | collective-permute-start | bytes 6488 | tf_op jit(solution)/shard_map/ppermute | solution.py:40
  260.3 2.2 collective-permute-start.32
  262.5 2.3 collective-permute-done.31
  264.8 4.4 %collective-permute-done.32 = f32[3,10,18,1]{3,2,1,0:T(8,128)S(1)} collective-permute-done((f32[3,10,18,1]{3,2,1,0:T(8,128)S(1)}, f32[3,10,18,1]{3,2,1,0:T(8,128)S(1)}, u32[]{:S(2)}, u32[]{:S(2)}) %collective-permute-start.32) | collective-permute-done | bytes 2192 | tf_op jit(solution)/shard_map/ppermute | solution.py:41
  276.6 1.6 collective-permute-start.33
  279.6 3.3 collective-permute-done.34
  285.6 3.1 collective-permute-done.36
  288.9 4.6 %collective-permute-start.37 = (f32[3,10,18,1]{3,2,1,0:T(8,128)S(1)}, f32[3,10,18,1]{3,2,1,0:T(8,128)S(1)}, u32[]{:S(2)}, u32[]{:S(2)}) collective-permute-start(f32[3,10,18,1]{3,2,1,0:T(8,128)S(1)} %get-tuple-element.208), channel_id=1, source_target_pairs={{0,1},{1,2},{2,3},{4,5},{5,6},{6,7},{8,9},{9,10},{10,11},{12,13},{... | collective-permute-start | bytes 6488 | tf_op jit(solution)/shard_map/ppermute | solution.py:40
  293.5 2.2 collective-permute-start.38
  295.8 2.2 collective-permute-done.37
  298.0 4.4 %collective-permute-done.38 = f32[3,10,18,1]{3,2,1,0:T(8,128)S(1)} collective-permute-done((f32[3,10,18,1]{3,2,1,0:T(8,128)S(1)}, f32[3,10,18,1]{3,2,1,0:T(8,128)S(1)}, u32[]{:S(2)}, u32[]{:S(2)}) %collective-permute-start.38) | collective-permute-done | bytes 2192 | tf_op jit(solution)/shard_map/ppermute | solution.py:41
  311.2 3.2 collective-permute-done.39
  315.7 3.1 collective-permute-done.40
  318.9 1.9 collective-permute-start.41
  320.9 6.8 %collective-permute-done.41 = f32[3,9,17,1]{3,2,1,0:T(8,128)S(1)} collective-permute-done((f32[3,9,17,1]{3,2,1,0:T(8,128)S(1)}, f32[3,9,17,1]{3,2,1,0:T(8,128)S(1)}, u32[]{:S(2)}, u32[]{:S(2)}) %collective-permute-start.41) | collective-permute-done | bytes 1868 | tf_op jit(solution)/shard_map/ppermute | solution.py:30
  328.7 1.8 fusion.221
  330.6 1.6 collective-permute-start.42
  333.5 3.2 collective-permute-done.43
  336.7 1.4 collective-permute-start.44
  340.6 1.9 collective-permute-done.45
  342.7 4.6 %collective-permute-start.46 = (f32[12,20,2]{2,1,0:T(8,128)S(1)}, f32[12,20,2]{2,1,0:T(8,128)S(1)}, u32[]{:S(2)}, u32[]{:S(2)}) collective-permute-start(f32[12,20,2]{2,1,0:T(8,128)S(1)} %get-tuple-element.263), channel_id=1, source_target_pairs={{0,1},{1,2},{2,3},{4,5},{5,6},{6,7},{8,9},{9,10},{10,11},{12,13},{... | collective-permute-start | bytes 5768 | tf_op jit(solution)/shard_map/ppermute | solution.py:40
  347.3 1.9 collective-permute-start.47
  349.4 4.4 %collective-permute-done.47 = f32[12,20,2]{2,1,0:T(8,128)S(1)} collective-permute-done((f32[12,20,2]{2,1,0:T(8,128)S(1)}, f32[12,20,2]{2,1,0:T(8,128)S(1)}, u32[]{:S(2)}, u32[]{:S(2)}) %collective-permute-start.47) | collective-permute-done | bytes 1952 | tf_op jit(solution)/shard_map/ppermute | solution.py:41
  (231 shorter events, 78.9 us)
Async XLA Ops:
  0.6 23.4 %copy-start.3 = (f32[3,8,16,128]{3,2,1,0:T(8,128)S(1)}, f32[3,8,16,128]{3,2,1,0:T(8,128)}, u32[]{:S(2)}) copy-start(f32[3,8,16,128]{3,2,1,0:T(8,128)} %param.2) | copy-start | bytes 589828
  1.4 7.6 %collective-permute-start = (f32[3,1,16,128]{3,2,1,0:T(8,128)S(1)}, f32[3,1,16,128]{3,2,1,0:T(8,128)S(1)}, u32[]{:S(2)}, u32[]{:S(2)}) collective-permute-start(f32[3,1,16,128]{3,2,1,0:T(8,128)S(1)} %slice.1434), channel_id=1, source_target_pairs={{8,0},{16,8},{24,16},{9,1},{17,9},{25,17},{10,2},{18,10},{26,18},{... | collective-permute-start | bytes 73736 | tf_op jit(solution)/shard_map/ppermute | solution.py:30
  3.4 14.2 %collective-permute-start.6 = (f32[1,16,128]{2,1,0:T(8,128)S(1)}, f32[1,16,128]{2,1,0:T(8,128)S(1)}, u32[]{:S(2)}, u32[]{:S(2)}) collective-permute-start(f32[1,16,128]{2,1,0:T(8,128)S(1)} %slice.1477), channel_id=1, source_target_pairs={{0,8},{8,16},{16,24},{1,9},{9,17},{17,25},{2,10},{10,18},{18,26},{... | collective-permute-start | bytes 24584 | tf_op jit(solution)/shard_map/ppermute | solution.py:30
  9.1 4.5 %collective-permute-start.1 = (f32[3,9,1,128]{3,2,1,0:T(1,128)S(1)}, f32[3,9,1,128]{3,2,1,0:T(1,128)S(1)}, u32[]{:S(2)}, u32[]{:S(2)}) collective-permute-start(f32[3,9,1,128]{3,2,1,0:T(1,128)S(1)} %slice.1813), channel_id=1, source_target_pairs={{4,0},{5,1},{6,2},{7,3},{12,8},{13,9},{14,10},{15,11},{20,16},{21,... | collective-permute-start | bytes 41480 | tf_op jit(solution)/shard_map/ppermute | solution.py:30
  13.6 10.4 %collective-permute-start.2 = (f32[3,9,17,1]{3,2,1,0:T(8,128)S(1)}, f32[3,9,17,1]{3,2,1,0:T(8,128)S(1)}, u32[]{:S(2)}, u32[]{:S(2)}) collective-permute-start(f32[3,9,17,1]{3,2,1,0:T(8,128)S(1)} %fusion), channel_id=1, source_target_pairs={{1,0},{2,1},{3,2},{5,4},{6,5},{7,6},{9,8},{10,9},{11,10},{13,12},{... | collective-permute-start | bytes 5516 | tf_op jit(solution)/shard_map/ppermute | solution.py:30
  25.6 80.7 %copy-start.13 = (f32[1,8,16,128]{3,2,1,0:T(8,128)}, f32[1,8,16,128]{3,2,1,0:T(8,128)S(1)}, u32[]{:S(2)}) copy-start(f32[1,8,16,128]{3,2,1,0:T(8,128)S(1)} %get-tuple-element.36) | copy-start | bytes 196612
  25.6 81.9 %copy-start.15 = (f32[1,8,16,128]{3,2,1,0:T(8,128)}, f32[1,8,16,128]{3,2,1,0:T(8,128)S(1)}, u32[]{:S(2)}) copy-start(f32[1,8,16,128]{3,2,1,0:T(8,128)S(1)} %get-tuple-element.37) | copy-start | bytes 196612
  25.6 83.9 %copy-start.17 = (f32[1,8,16,128]{3,2,1,0:T(8,128)}, f32[1,8,16,128]{3,2,1,0:T(8,128)S(1)}, u32[]{:S(2)}) copy-start(f32[1,8,16,128]{3,2,1,0:T(8,128)S(1)} %get-tuple-element.38) | copy-start | bytes 196612
  25.6 98.7 %copy-start.5 = (f32[9,16,128]{2,1,0:T(8,128)}, f32[9,16,128]{2,1,0:T(8,128)S(1)}, u32[]{:S(2)}) copy-start(f32[9,16,128]{2,1,0:T(8,128)S(1)} %get-tuple-element.273) | copy-start | bytes 221188
  107.6 17.7 %copy-start.7 = (f32[1,8,16,128]{3,2,1,0:T(8,128)}, f32[1,8,16,128]{3,2,1,0:T(8,128)S(1)}, u32[]{:S(2)}) copy-start(f32[1,8,16,128]{3,2,1,0:T(8,128)S(1)} %get-tuple-element.28) | copy-start | bytes 196612
  108.8 16.4 %copy-start.9 = (f32[1,8,16,128]{3,2,1,0:T(8,128)}, f32[1,8,16,128]{3,2,1,0:T(8,128)S(1)}, u32[]{:S(2)}) copy-start(f32[1,8,16,128]{3,2,1,0:T(8,128)S(1)} %get-tuple-element.26) | copy-start | bytes 196612
  110.8 14.5 %copy-start.11 = (f32[1,8,16,128]{3,2,1,0:T(8,128)}, f32[1,8,16,128]{3,2,1,0:T(8,128)S(1)}, u32[]{:S(2)}) copy-start(f32[1,8,16,128]{3,2,1,0:T(8,128)S(1)} %get-tuple-element.22) | copy-start | bytes 196612
  110.8 6.6 %collective-permute-start.7 = (f32[9,1,128]{2,1,0:T(1,128)S(1)}, f32[9,1,128]{2,1,0:T(1,128)S(1)}, u32[]{:S(2)}, u32[]{:S(2)}) collective-permute-start(f32[9,1,128]{2,1,0:T(1,128)S(1)} %slice.1852), channel_id=1, source_target_pairs={{0,4},{1,5},{2,6},{3,7},{8,12},{9,13},{10,14},{11,15},{16,20},{17,... | collective-permute-start | bytes 13832 | tf_op jit(solution)/shard_map/ppermute | solution.py:30
  114.1 8.5 %collective-permute-start.3 = (f32[9,1,16,128]{3,2,1,0:T(8,128)S(1)}, f32[9,1,16,128]{3,2,1,0:T(8,128)S(1)}, u32[]{:S(2)}, u32[]{:S(2)}) collective-permute-start(f32[9,1,16,128]{3,2,1,0:T(8,128)S(1)} %slice.1832), channel_id=1, source_target_pairs={{0,8},{8,16},{16,24},{1,9},{9,17},{17,25},{2,10},{10,18},{18,26},{... | collective-permute-start | bytes 221192 | tf_op jit(solution)/shard_map/ppermute | solution.py:30
  117.5 7.8 %copy-start.24 = (f32[9,1,128]{2,1,0:T(1,128)}, f32[9,1,128]{2,1,0:T(1,128)S(1)}, u32[]{:S(2)}) copy-start(f32[9,1,128]{2,1,0:T(1,128)S(1)} %collective-permute-done.7) | copy-start | bytes 13828
  117.6 6.8 %collective-permute-start.8 = (f32[9,17,1]{2,1,0:T(8,128)S(1)}, f32[9,17,1]{2,1,0:T(8,128)S(1)}, u32[]{:S(2)}, u32[]{:S(2)}) collective-permute-start(f32[9,17,1]{2,1,0:T(8,128)S(1)} %fusion.185), channel_id=1, source_target_pairs={{0,1},{1,2},{2,3},{4,5},{5,6},{6,7},{8,9},{9,10},{10,11},{12,13},{... | collective-permute-start | bytes 1844 | tf_op jit(solution)/shard_map/ppermute | solution.py:30
  122.6 11.1 %copy-start.4 = (f32[9,1,16,128]{3,2,1,0:T(8,128)}, f32[9,1,16,128]{3,2,1,0:T(8,128)S(1)}, u32[]{:S(2)}) copy-start(f32[9,1,16,128]{3,2,1,0:T(8,128)S(1)} %collective-permute-done.3) | copy-start | bytes 221188
  122.7 2.6 collective-permute-start.4
  126.3 6.0 %collective-permute-start.5 = (f32[9,9,17,1]{2,3,1,0:T(1,128)S(1)}, f32[9,9,17,1]{2,3,1,0:T(1,128)S(1)}, u32[]{:S(2)}, u32[]{:S(2)}) collective-permute-start(f32[9,9,17,1]{2,3,1,0:T(1,128)S(1)} %copy.434), channel_id=1, source_target_pairs={{0,1},{1,2},{2,3},{4,5},{5,6},{6,7},{8,9},{9,10},{10,11},{12,13},{... | collective-permute-start | bytes 16532 | tf_op jit(solution)/shard_map/ppermute | solution.py:30
  132.9 0.9 copy-start.22
  132.9 1.0 copy-start.23
  135.1 22.0 %copy-start.6 = (f32[9,16,128]{2,1,0:T(8,128)S(1)}, f32[9,16,128]{2,1,0:T(8,128)}, u32[]{:S(2)}) copy-start(f32[9,16,128]{2,1,0:T(8,128)} %copy-done.5) | copy-start | bytes 221188
  135.1 22.0 %copy-start.25 = (f32[9,1,128]{2,1,0:T(1,128)S(1)}, f32[9,1,128]{2,1,0:T(1,128)}, u32[]{:S(2)}) copy-start(f32[9,1,128]{2,1,0:T(1,128)} %copy-done.24) | copy-start | bytes 13828
  135.1 22.1 %copy-start.20 = (f32[9,17,1]{2,1,0:T(8,128)S(1)}, f32[9,17,1]{2,1,0:T(8,128)}, u32[]{:S(2)}) copy-start(f32[9,17,1]{2,1,0:T(8,128)} %copy-done.19) | copy-start | bytes 1840
  135.1 5.4 %collective-permute-start.10 = (f32[3,1,16,128]{3,2,1,0:T(8,128)S(1)}, f32[3,1,16,128]{3,2,1,0:T(8,128)S(1)}, u32[]{:S(2)}, u32[]{:S(2)}) collective-permute-start(f32[3,1,16,128]{3,2,1,0:T(8,128)S(1)} %get-tuple-element.247), channel_id=1, source_target_pairs={{8,0},{16,8},{24,16},{9,1},{17,9},{25,17},{10,2},{18,10},{26,18},{... | collective-permute-start | bytes 73736 | tf_op jit(solution)/shard_map/ppermute | solution.py:41
  136.5 4.9 %collective-permute-start.9 = (f32[3,1,16,128]{3,2,1,0:T(8,128)S(1)}, f32[3,1,16,128]{3,2,1,0:T(8,128)S(1)}, u32[]{:S(2)}, u32[]{:S(2)}) collective-permute-start(f32[3,1,16,128]{3,2,1,0:T(8,128)S(1)} %get-tuple-element.246), channel_id=1, source_target_pairs={{0,8},{8,16},{16,24},{1,9},{9,17},{17,25},{2,10},{10,18},{18,26},{... | collective-permute-start | bytes 73736 | tf_op jit(solution)/shard_map/ppermute | solution.py:40
  141.5 3.8 %collective-permute-start.11 = (f32[3,10,1,128]{3,2,1,0:T(1,128)S(1)}, f32[3,10,1,128]{3,2,1,0:T(1,128)S(1)}, u32[]{:S(2)}, u32[]{:S(2)}) collective-permute-start(f32[3,10,1,128]{3,2,1,0:T(1,128)S(1)} %get-tuple-element.236), channel_id=1, source_target_pairs={{0,4},{1,5},{2,6},{3,7},{8,12},{9,13},{10,14},{11,15},{16,20},{17,... | collective-permute-start | bytes 46088 | tf_op jit(solution)/shard_map/ppermute | solution.py:40
  144.0 4.5 %collective-permute-start.12 = (f32[3,10,1,128]{3,2,1,0:T(1,128)S(1)}, f32[3,10,1,128]{3,2,1,0:T(1,128)S(1)}, u32[]{:S(2)}, u32[]{:S(2)}) collective-permute-start(f32[3,10,1,128]{3,2,1,0:T(1,128)S(1)} %get-tuple-element.237), channel_id=1, source_target_pairs={{4,0},{5,1},{6,2},{7,3},{12,8},{13,9},{14,10},{15,11},{20,16},{21,... | collective-permute-start | bytes 46088 | tf_op jit(solution)/shard_map/ppermute | solution.py:41
  148.7 10.4 %collective-permute-start.13 = (f32[3,10,18,1]{3,2,1,0:T(8,128)S(1)}, f32[3,10,18,1]{3,2,1,0:T(8,128)S(1)}, u32[]{:S(2)}, u32[]{:S(2)}) collective-permute-start(f32[3,10,18,1]{3,2,1,0:T(8,128)S(1)} %get-tuple-element.216), channel_id=1, source_target_pairs={{0,1},{1,2},{2,3},{4,5},{5,6},{6,7},{8,9},{9,10},{10,11},{12,13},{... | collective-permute-start | bytes 6488 | tf_op jit(solution)/shard_map/ppermute | solution.py:40
  154.6 8.8 %collective-permute-start.14 = (f32[3,10,18,1]{3,2,1,0:T(8,128)S(1)}, f32[3,10,18,1]{3,2,1,0:T(8,128)S(1)}, u32[]{:S(2)}, u32[]{:S(2)}) collective-permute-start(f32[3,10,18,1]{3,2,1,0:T(8,128)S(1)} %get-tuple-element.217), channel_id=1, source_target_pairs={{1,0},{2,1},{3,2},{5,4},{6,5},{7,6},{9,8},{10,9},{11,10},{13,12},{... | collective-permute-start | bytes 6488 | tf_op jit(solution)/shard_map/ppermute | solution.py:41
  171.3 5.2 %collective-permute-start.15 = (f32[3,1,16,128]{3,2,1,0:T(8,128)S(1)}, f32[3,1,16,128]{3,2,1,0:T(8,128)S(1)}, u32[]{:S(2)}, u32[]{:S(2)}) collective-permute-start(f32[3,1,16,128]{3,2,1,0:T(8,128)S(1)} %get-tuple-element.244), channel_id=1, source_target_pairs={{0,8},{8,16},{16,24},{1,9},{9,17},{17,25},{2,10},{10,18},{18,26},{... | collective-permute-start | bytes 73736 | tf_op jit(solution)/shard_map/ppermute | solution.py:40
  175.2 4.9 %collective-permute-start.16 = (f32[3,1,16,128]{3,2,1,0:T(8,128)S(1)}, f32[3,1,16,128]{3,2,1,0:T(8,128)S(1)}, u32[]{:S(2)}, u32[]{:S(2)}) collective-permute-start(f32[3,1,16,128]{3,2,1,0:T(8,128)S(1)} %get-tuple-element.245), channel_id=1, source_target_pairs={{8,0},{16,8},{24,16},{9,1},{17,9},{25,17},{10,2},{18,10},{26,18},{... | collective-permute-start | bytes 73736 | tf_op jit(solution)/shard_map/ppermute | solution.py:41
  180.1 2.7 collective-permute-start.17
  181.5 4.5 %collective-permute-start.18 = (f32[3,10,1,128]{3,2,1,0:T(1,128)S(1)}, f32[3,10,1,128]{3,2,1,0:T(1,128)S(1)}, u32[]{:S(2)}, u32[]{:S(2)}) collective-permute-start(f32[3,10,1,128]{3,2,1,0:T(1,128)S(1)} %get-tuple-element.235), channel_id=1, source_target_pairs={{4,0},{5,1},{6,2},{7,3},{12,8},{13,9},{14,10},{15,11},{20,16},{21,... | collective-permute-start | bytes 46088 | tf_op jit(solution)/shard_map/ppermute | solution.py:41
  186.2 8.8 %collective-permute-start.19 = (f32[3,10,18,1]{3,2,1,0:T(8,128)S(1)}, f32[3,10,18,1]{3,2,1,0:T(8,128)S(1)}, u32[]{:S(2)}, u32[]{:S(2)}) collective-permute-start(f32[3,10,18,1]{3,2,1,0:T(8,128)S(1)} %get-tuple-element.214), channel_id=1, source_target_pairs={{0,1},{1,2},{2,3},{4,5},{5,6},{6,7},{8,9},{9,10},{10,11},{12,13},{... | collective-permute-start | bytes 6488 | tf_op jit(solution)/shard_map/ppermute | solution.py:40
  190.5 8.8 %collective-permute-start.20 = (f32[3,10,18,1]{3,2,1,0:T(8,128)S(1)}, f32[3,10,18,1]{3,2,1,0:T(8,128)S(1)}, u32[]{:S(2)}, u32[]{:S(2)}) collective-permute-start(f32[3,10,18,1]{3,2,1,0:T(8,128)S(1)} %get-tuple-element.215), channel_id=1, source_target_pairs={{1,0},{2,1},{3,2},{5,4},{6,5},{7,6},{9,8},{10,9},{11,10},{13,12},{... | collective-permute-start | bytes 6488 | tf_op jit(solution)/shard_map/ppermute | solution.py:41
  206.8 4.9 %collective-permute-start.21 = (f32[3,1,16,128]{3,2,1,0:T(8,128)S(1)}, f32[3,1,16,128]{3,2,1,0:T(8,128)S(1)}, u32[]{:S(2)}, u32[]{:S(2)}) collective-permute-start(f32[3,1,16,128]{3,2,1,0:T(8,128)S(1)} %get-tuple-element.242), channel_id=1, source_target_pairs={{0,8},{8,16},{16,24},{1,9},{9,17},{17,25},{2,10},{10,18},{18,26},{... | collective-permute-start | bytes 73736 | tf_op jit(solution)/shard_map/ppermute | solution.py:40
  210.4 4.6 %collective-permute-start.22 = (f32[3,1,16,128]{3,2,1,0:T(8,128)S(1)}, f32[3,1,16,128]{3,2,1,0:T(8,128)S(1)}, u32[]{:S(2)}, u32[]{:S(2)}) collective-permute-start(f32[3,1,16,128]{3,2,1,0:T(8,128)S(1)} %get-tuple-element.243), channel_id=1, source_target_pairs={{8,0},{16,8},{24,16},{9,1},{17,9},{25,17},{10,2},{18,10},{26,18},{... | collective-permute-start | bytes 73736 | tf_op jit(solution)/shard_map/ppermute | solution.py:41
  215.0 2.7 collective-permute-start.23
  216.4 4.5 %collective-permute-start.24 = (f32[3,10,1,128]{3,2,1,0:T(1,128)S(1)}, f32[3,10,1,128]{3,2,1,0:T(1,128)S(1)}, u32[]{:S(2)}, u32[]{:S(2)}) collective-permute-start(f32[3,10,1,128]{3,2,1,0:T(1,128)S(1)} %get-tuple-element.233), channel_id=1, source_target_pairs={{4,0},{5,1},{6,2},{7,3},{12,8},{13,9},{14,10},{15,11},{20,16},{21,... | collective-permute-start | bytes 46088 | tf_op jit(solution)/shard_map/ppermute | solution.py:41
  221.1 9.0 %collective-permute-start.25 = (f32[3,10,18,1]{3,2,1,0:T(8,128)S(1)}, f32[3,10,18,1]{3,2,1,0:T(8,128)S(1)}, u32[]{:S(2)}, u32[]{:S(2)}) collective-permute-start(f32[3,10,18,1]{3,2,1,0:T(8,128)S(1)} %get-tuple-element.212), channel_id=1, source_target_pairs={{0,1},{1,2},{2,3},{4,5},{5,6},{6,7},{8,9},{9,10},{10,11},{12,13},{... | collective-permute-start | bytes 6488 | tf_op jit(solution)/shard_map/ppermute | solution.py:40
  225.7 8.8 %collective-permute-start.26 = (f32[3,10,18,1]{3,2,1,0:T(8,128)S(1)}, f32[3,10,18,1]{3,2,1,0:T(8,128)S(1)}, u32[]{:S(2)}, u32[]{:S(2)}) collective-permute-start(f32[3,10,18,1]{3,2,1,0:T(8,128)S(1)} %get-tuple-element.213), channel_id=1, source_target_pairs={{1,0},{2,1},{3,2},{5,4},{6,5},{7,6},{9,8},{10,9},{11,10},{13,12},{... | collective-permute-start | bytes 6488 | tf_op jit(solution)/shard_map/ppermute | solution.py:41
  242.0 4.3 %collective-permute-start.27 = (f32[3,1,16,128]{3,2,1,0:T(8,128)S(1)}, f32[3,1,16,128]{3,2,1,0:T(8,128)S(1)}, u32[]{:S(2)}, u32[]{:S(2)}) collective-permute-start(f32[3,1,16,128]{3,2,1,0:T(8,128)S(1)} %get-tuple-element.240), channel_id=1, source_target_pairs={{0,8},{8,16},{16,24},{1,9},{9,17},{17,25},{2,10},{10,18},{18,26},{... | collective-permute-start | bytes 73736 | tf_op jit(solution)/shard_map/ppermute | solution.py:40
  245.0 4.6 %collective-permute-start.28 = (f32[3,1,16,128]{3,2,1,0:T(8,128)S(1)}, f32[3,1,16,128]{3,2,1,0:T(8,128)S(1)}, u32[]{:S(2)}, u32[]{:S(2)}) collective-permute-start(f32[3,1,16,128]{3,2,1,0:T(8,128)S(1)} %get-tuple-element.241), channel_id=1, source_target_pairs={{8,0},{16,8},{24,16},{9,1},{17,9},{25,17},{10,2},{18,10},{26,18},{... | collective-permute-start | bytes 73736 | tf_op jit(solution)/shard_map/ppermute | solution.py:41
  249.6 2.7 collective-permute-start.29
  251.0 4.5 %collective-permute-start.30 = (f32[3,10,1,128]{3,2,1,0:T(1,128)S(1)}, f32[3,10,1,128]{3,2,1,0:T(1,128)S(1)}, u32[]{:S(2)}, u32[]{:S(2)}) collective-permute-start(f32[3,10,1,128]{3,2,1,0:T(1,128)S(1)} %get-tuple-element.231), channel_id=1, source_target_pairs={{4,0},{5,1},{6,2},{7,3},{12,8},{13,9},{14,10},{15,11},{20,16},{21,... | collective-permute-start | bytes 46088 | tf_op jit(solution)/shard_map/ppermute | solution.py:41
  255.7 9.0 %collective-permute-start.31 = (f32[3,10,18,1]{3,2,1,0:T(8,128)S(1)}, f32[3,10,18,1]{3,2,1,0:T(8,128)S(1)}, u32[]{:S(2)}, u32[]{:S(2)}) collective-permute-start(f32[3,10,18,1]{3,2,1,0:T(8,128)S(1)} %get-tuple-element.210), channel_id=1, source_target_pairs={{0,1},{1,2},{2,3},{4,5},{5,6},{6,7},{8,9},{9,10},{10,11},{12,13},{... | collective-permute-start | bytes 6488 | tf_op jit(solution)/shard_map/ppermute | solution.py:40
  260.3 8.8 %collective-permute-start.32 = (f32[3,10,18,1]{3,2,1,0:T(8,128)S(1)}, f32[3,10,18,1]{3,2,1,0:T(8,128)S(1)}, u32[]{:S(2)}, u32[]{:S(2)}) collective-permute-start(f32[3,10,18,1]{3,2,1,0:T(8,128)S(1)} %get-tuple-element.211), channel_id=1, source_target_pairs={{1,0},{2,1},{3,2},{5,4},{6,5},{7,6},{9,8},{10,9},{11,10},{13,12},{... | collective-permute-start | bytes 6488 | tf_op jit(solution)/shard_map/ppermute | solution.py:41
  276.6 3.0 collective-permute-start.33
  278.3 4.6 %collective-permute-start.34 = (f32[3,1,16,128]{3,2,1,0:T(8,128)S(1)}, f32[3,1,16,128]{3,2,1,0:T(8,128)S(1)}, u32[]{:S(2)}, u32[]{:S(2)}) collective-permute-start(f32[3,1,16,128]{3,2,1,0:T(8,128)S(1)} %get-tuple-element.239), channel_id=1, source_target_pairs={{8,0},{16,8},{24,16},{9,1},{17,9},{25,17},{10,2},{18,10},{26,18},{... | collective-permute-start | bytes 73736 | tf_op jit(solution)/shard_map/ppermute | solution.py:41
  282.9 2.7 collective-permute-start.35
  284.2 4.5 %collective-permute-start.36 = (f32[3,10,1,128]{3,2,1,0:T(1,128)S(1)}, f32[3,10,1,128]{3,2,1,0:T(1,128)S(1)}, u32[]{:S(2)}, u32[]{:S(2)}) collective-permute-start(f32[3,10,1,128]{3,2,1,0:T(1,128)S(1)} %get-tuple-element.229), channel_id=1, source_target_pairs={{4,0},{5,1},{6,2},{7,3},{12,8},{13,9},{14,10},{15,11},{20,16},{21,... | collective-permute-start | bytes 46088 | tf_op jit(solution)/shard_map/ppermute | solution.py:41
  288.9 9.0 %collective-permute-start.37 = (f32[3,10,18,1]{3,2,1,0:T(8,128)S(1)}, f32[3,10,18,1]{3,2,1,0:T(8,128)S(1)}, u32[]{:S(2)}, u32[]{:S(2)}) collective-permute-start(f32[3,10,18,1]{3,2,1,0:T(8,128)S(1)} %get-tuple-element.208), channel_id=1, source_target_pairs={{0,1},{1,2},{2,3},{4,5},{5,6},{6,7},{8,9},{9,10},{10,11},{12,13},{... | collective-permute-start | bytes 6488 | tf_op jit(solution)/shard_map/ppermute | solution.py:40
  293.5 8.8 %collective-permute-start.38 = (f32[3,10,18,1]{3,2,1,0:T(8,128)S(1)}, f32[3,10,18,1]{3,2,1,0:T(8,128)S(1)}, u32[]{:S(2)}, u32[]{:S(2)}) collective-permute-start(f32[3,10,18,1]{3,2,1,0:T(8,128)S(1)} %get-tuple-element.209), channel_id=1, source_target_pairs={{1,0},{2,1},{3,2},{5,4},{6,5},{7,6},{9,8},{10,9},{11,10},{13,12},{... | collective-permute-start | bytes 6488 | tf_op jit(solution)/shard_map/ppermute | solution.py:41
  309.8 18.3 %copy-start = (f32[3,8,16,128]{3,2,1,0:T(8,128)}, f32[3,8,16,128]{3,2,1,0:T(8,128)S(1)}, u32[]{:S(2)}) copy-start(f32[3,8,16,128]{3,2,1,0:T(8,128)S(1)} %fusion.32) | copy-start | bytes 589828
  309.8 4.6 %collective-permute-start.39 = (f32[3,1,16,128]{3,2,1,0:T(8,128)S(1)}, f32[3,1,16,128]{3,2,1,0:T(8,128)S(1)}, u32[]{:S(2)}, u32[]{:S(2)}) collective-permute-start(f32[3,1,16,128]{3,2,1,0:T(8,128)S(1)} %slice.2088), channel_id=1, source_target_pairs={{8,0},{16,8},{24,16},{9,1},{17,9},{25,17},{10,2},{18,10},{26,18},{... | collective-permute-start | bytes 73736 | tf_op jit(solution)/shard_map/ppermute | solution.py:30
  314.4 4.5 %collective-permute-start.40 = (f32[3,9,1,128]{3,2,1,0:T(1,128)S(1)}, f32[3,9,1,128]{3,2,1,0:T(1,128)S(1)}, u32[]{:S(2)}, u32[]{:S(2)}) collective-permute-start(f32[3,9,1,128]{3,2,1,0:T(1,128)S(1)} %pad_maximum_fusion.58), channel_id=1, source_target_pairs={{4,0},{5,1},{6,2},{7,3},{12,8},{13,9},{14,10},{15,11},{20,16},{21,... | collective-permute-start | bytes 41480 | tf_op jit(solution)/shard_map/ppermute | solution.py:30
  318.9 8.8 %collective-permute-start.41 = (f32[3,9,17,1]{3,2,1,0:T(8,128)S(1)}, f32[3,9,17,1]{3,2,1,0:T(8,128)S(1)}, u32[]{:S(2)}, u32[]{:S(2)}) collective-permute-start(f32[3,9,17,1]{3,2,1,0:T(8,128)S(1)} %bitcast.173), channel_id=1, source_target_pairs={{1,0},{2,1},{3,2},{5,4},{6,5},{7,6},{9,8},{10,9},{11,10},{13,12},{... | collective-permute-start | bytes 5516 | tf_op jit(solution)/shard_map/ppermute | solution.py:30
  330.6 3.0 collective-permute-start.42
  332.2 4.5 %collective-permute-start.43 = (f32[2,16,128]{2,1,0:T(8,128)S(1)}, f32[2,16,128]{2,1,0:T(8,128)S(1)}, u32[]{:S(2)}, u32[]{:S(2)}) collective-permute-start(f32[2,16,128]{2,1,0:T(8,128)S(1)} %get-tuple-element.272), channel_id=1, source_target_pairs={{8,0},{16,8},{24,16},{9,1},{17,9},{25,17},{10,2},{18,10},{26,18},{... | collective-permute-start | bytes 49160 | tf_op jit(solution)/shard_map/ppermute | solution.py:41
  336.7 3.9 %collective-permute-start.44 = (f32[12,2,128]{2,1,0:T(2,128)S(1)}, f32[12,2,128]{2,1,0:T(2,128)S(1)}, u32[]{:S(2)}, u32[]{:S(2)}) collective-permute-start(f32[12,2,128]{2,1,0:T(2,128)S(1)} %get-tuple-element.269), channel_id=1, source_target_pairs={{0,4},{1,5},{2,6},{3,7},{8,12},{9,13},{10,14},{11,15},{16,20},{17,... | collective-permute-start | bytes 36872 | tf_op jit(solution)/shard_map/ppermute | solution.py:40
  338.1 4.4 %collective-permute-start.45 = (f32[12,2,128]{2,1,0:T(2,128)S(1)}, f32[12,2,128]{2,1,0:T(2,128)S(1)}, u32[]{:S(2)}, u32[]{:S(2)}) collective-permute-start(f32[12,2,128]{2,1,0:T(2,128)S(1)} %get-tuple-element.270), channel_id=1, source_target_pairs={{4,0},{5,1},{6,2},{7,3},{12,8},{13,9},{14,10},{15,11},{20,16},{21,... | collective-permute-start | bytes 36872 | tf_op jit(solution)/shard_map/ppermute | solution.py:41
  342.7 6.7 %collective-permute-start.46 = (f32[12,20,2]{2,1,0:T(8,128)S(1)}, f32[12,20,2]{2,1,0:T(8,128)S(1)}, u32[]{:S(2)}, u32[]{:S(2)}) collective-permute-start(f32[12,20,2]{2,1,0:T(8,128)S(1)} %get-tuple-element.263), channel_id=1, source_target_pairs={{0,1},{1,2},{2,3},{4,5},{5,6},{6,7},{8,9},{9,10},{10,11},{12,13},{... | collective-permute-start | bytes 5768 | tf_op jit(solution)/shard_map/ppermute | solution.py:40
  347.3 6.5 %collective-permute-start.47 = (f32[12,20,2]{2,1,0:T(8,128)S(1)}, f32[12,20,2]{2,1,0:T(8,128)S(1)}, u32[]{:S(2)}, u32[]{:S(2)}) collective-permute-start(f32[12,20,2]{2,1,0:T(8,128)S(1)} %get-tuple-element.264), channel_id=1, source_target_pairs={{1,0},{2,1},{3,2},{5,4},{6,5},{7,6},{9,8},{10,9},{11,10},{13,12},{... | collective-permute-start | bytes 5768 | tf_op jit(solution)/shard_map/ppermute | solution.py:41
  (10 other events, 8.8 us)
where the time goes:
time: 363 us; the launch traced here: 357 us
  starting transfers between devices  117 us (32%)
  waiting for transfers between devices  95.1 us (26%)
  blocking collectives  77.5 us (21%)
  other arithmetic  45.8 us (13%)
  local copies, waits for them, and re-layouts  16.5 us (5%)
  between operations  5.04 us (1%)
    ppermute x18, waiting for transfers between devices, extended(): after = lax.ppermute(leading, axis, down)  60.5 us
    ppermute x18, starting transfers between devices, extended(): before = lax.ppermute(last, axis, up)  55.8 us
    psum x1, blocking collectives, on_device(): total = lax.psum(jnp.sum(jnp.exp(score - top)), ('gx', 'gy', 'gz'))  40.4 us
    pmax x1, blocking collectives, on_device(): top = lax.pmax(local_top, ('gx', 'gy', 'gz'))  37 us
    ppermute x12, starting transfers between devices, passed_along(): return lax.ppermute(block, axis, route)  32.3 us
    ppermute x18, starting transfers between devices, extended(): after = lax.ppermute(leading, axis, down)  28.6 us
    ppermute x12, waiting for transfers between devices, passed_along(): return lax.ppermute(block, axis, route)  22.9 us
    ppermute x18, waiting for transfers between devices, extended(): before = lax.ppermute(last, axis, up)  11.7 us
  transfers between devices with their start and end apart: 48, of which 30 were waited for; matrix products, arithmetic and copies ran while one was open for 2% of the time, Pallas kernels for 0%

commit v1 on v0

v1 whole, which is shorter than its diff:
```python
import functools
import math

import jax
import jax.numpy as jnp
from jax import lax
from jax.experimental import pallas as pl
from jax.experimental.pallas import tpu as pltpu
from jax.sharding import PartitionSpec as P

ITERS = 6
lame = 0.3 / (1.3 * 0.4)
shear = 1.0 / 2.6
power_scale = 3.0
damping = 0.6
shift_term = 0.1
diag_factor = (lame + 3.0 * shear) / 16.0
FACE = 2.5 - math.sqrt(2.0)
DIAGONAL = 2.5 - math.sqrt(3.0)
MESH = pl.DeviceIdType.MESH
D = 8
C = 16


def gather_kernel(u_ref, rho_ref, out, pack, zs, zr, xs, xr, ys, yr):
    ix, iy, iz = (lax.axis_index(a) for a in ("gx", "gy", "gz"))
    nx, ny, nz = (lax.axis_size(a) for a in ("gx", "gy", "gz"))
    lx, ly, lz = rho_ref.shape
    group = lx + 2
    lane = lax.broadcasted_iota(jnp.int32, (ly, lz), 1)
    for c in range(4):
        first = jnp.zeros((ly, lz), jnp.float32)
        last = first
        for x in range(lx):
            tile = u_ref[c, x] if c < 3 else rho_ref[x]
            out[2 + x, c, 0:ly] = tile
            here = (lane >= C * x) & (lane < C * x + C)
            first = jnp.where(here, pltpu.roll(tile, C * x, 1) if x else tile, first)
            last = jnp.where(here, pltpu.roll(tile, (C * x + C) % lz, 1), last)
        pack[0, c] = first
        pack[1, c] = last

    def send(src, dst, ssem, rsem, axis, target):
        return pltpu.make_async_remote_copy(
            src_ref=src, dst_ref=dst, send_sem=ssem, recv_sem=rsem,
            device_id={axis: target}, device_id_type=MESH)

    def phase(axis, index, count, items):
        for step, src, dst, ssem, rsem in items:
            @pl.when((index + step >= 0) & (index + step < count))
            def _(step=step, src=src, dst=dst, ssem=ssem, rsem=rsem):
                send(src, dst, ssem, rsem, axis, index + step).start()
        for step, src, dst, ssem, rsem in items:
            has = (index - step >= 0) & (index - step < count)

            @pl.when(jnp.logical_not(has))
            def _(dst=dst):
                dst[...] = jnp.zeros(dst.shape, jnp.float32)

            @pl.when(has)
            def _(step=step, src=src, dst=dst, ssem=ssem, rsem=rsem):
                send(src, dst, ssem, rsem, axis, index - step).wait_recv()
        for step, src, dst, ssem, rsem in items:
            @pl.when((index + step >= 0) & (index + step < count))
            def _(step=step, src=src, dst=dst, ssem=ssem, rsem=rsem):
                send(src, dst, ssem, rsem, axis, index + step).wait_send()

    own = pl.ds(0, ly)
    phase("gz", iz, nz, [
        (-1, pack.at[0], out.at[0, :, own], zs.at[0], zr.at[0]),
        (1, pack.at[1], out.at[1, :, own], zs.at[1], zr.at[1]),
    ])
    phase("gx", ix, nx, [
        (1, out.at[pl.ds(0, group), :, own], out.at[pl.ds(group, group), :, own], xs.at[0], xr.at[0]),
        (-1, out.at[pl.ds(0, group), :, own], out.at[pl.ds(2 * group, group), :, own], xs.at[1], xr.at[1]),
        (-2, out.at[pl.ds(0, 3), :, own], out.at[pl.ds(3 * group, 3), :, own], xs.at[2], xr.at[2]),
    ])
    phase("gy", iy, ny, [
        (1, out.at[:, :, pl.ds(ly - D, D)], out.at[:, :, pl.ds(2 * ly, D)], ys.at[0], yr.at[0]),
        (-1, out.at[:, :, pl.ds(0, ly)], out.at[:, :, pl.ds(ly, ly)], ys.at[1], yr.at[1]),
    ])


def up(v, axis):
    return pltpu.roll(v, v.shape[axis] - 1, axis)


def down(v, axis):
    return pltpu.roll(v, 1, axis)


def raw_strain(low, high):
    g = []
    for c in range(3):
        s = low[c] + high[c]
        d = high[c] - low[c]
        s1, d1 = up(s, 1), up(d, 1)
        za, zd, xd = s + s1, s1 - s, d + d1
        g.append((xd + up(xd, 0), up(za, 0) - za, zd + up(zd, 0)))
    return (g[0][0], g[1][1], g[2][2], g[1][0] + g[0][1], g[2][1] + g[1][2], g[0][2] + g[2][0])


def cmul(t):
    tr = lame * (t[0] + t[1] + t[2])
    return [tr + (2.0 * shear) * t[i] for i in range(3)] + [shear * t[i] for i in range(3, 6)]


ROWS = ((0, 3, 5), (3, 1, 4), (5, 4, 2))


def gather_forces(a, b):
    out = []
    for c in range(3):
        i, j, k = ROWS[c]
        x = a[i] - b[i]
        y = a[j] + b[j]
        z = a[k] + b[k]
        w = down(x + y, 0) + (x - y)
        v = down(z, 0) + z
        out.append(down(w + v, 1) + (w - v))
    return out


def compute_kernel(place, ext, adj_out, sens_out, stat, U, RHO, B, VM, JB, S, LOAD, DM, K16, A, Q):
    lx, ly, lz = sens_out.shape
    nx, ny, nz = place[3], place[4], place[5]
    group = lx + 2
    X = lx + 2 * D
    rows, lanes = ly + 2 * D, 2 * lz
    lane = lax.broadcasted_iota(jnp.int32, (2 * ly + D, lz), 1)
    for t in range(X + 1):
        g, xi = divmod(t, lx)
        base = (group, 0, 2 * group, 3 * group)[g]
        for c in range(4):
            if c == 3 and t == X:
                continue
            main = ext[base + 2 + xi, c]
            above = ext[base, c]
            below = ext[base + 1, c]
            if xi:
                above = pltpu.roll(above, lz - C * xi, 1)
            if (lz - C - C * xi) % lz:
                below = pltpu.roll(below, (lz - C - C * xi) % lz, 1)
            if c < 3:
                side = jnp.where(lane < D + 1, above, jnp.where(lane >= lz - D, below, 0.0))
                U[t, c, :, 0:lz] = main
                U[t, c, :, lz:lanes] = side
            else:
                side = jnp.where(lane < D, above, jnp.where(lane >= lz - D, below, 0.0))
                for lo, hi, to in ((0, ly + D, 0), (2 * ly, 2 * ly + D, ly + D)):
                    RHO[t, to:to + hi - lo, 0:lz] = main[lo:hi]
                    RHO[t, to:to + hi - lo, lz:lanes] = side[lo:hi]

    def cut(v):
        return jnp.concatenate([v[0:ly + D], v[2 * ly:2 * ly + D]], axis=0)

    def stage_one(t, best):
        low = [U[t, c] for c in range(3)]
        high = [U[t + 1, c] for c in range(3)]
        b = cmul([cut(0.25 * e) for e in raw_strain(low, high)])
        j = (b[0] * b[0] + b[1] * b[1] + b[2] * b[2] - b[0] * b[1] - b[1] * b[2] - b[2] * b[0]
             + 3.0 * (b[3] * b[3] + b[4] * b[4] + b[5] * b[5]))
        rho = RHO[t]
        vm = jnp.sqrt(rho * j + 1.0)
        for i in range(6):
            B[t, i] = b[i]
        JB[t] = j
        VM[t] = vm
        K16[t] = jnp.where(rho > 0.0, (0.01 + 0.99 * (rho * rho * rho)) * 0.0625, 0.0)
        return jnp.maximum(best, vm)

    best = lax.fori_loop(0, X, stage_one, jnp.ones((rows, lanes), jnp.float32))
    top = power_scale * jnp.max(best)

    def stage_two(t, _):
        vm = VM[t]
        weight = jnp.exp(power_scale * vm - top)
        factor = weight / (2.0 * vm)
        f = factor * RHO[t] * (0.5 * shear)
        b = [B[t, i] for i in range(6)]
        tr = b[0] + b[1] + b[2]
        for i in range(3):
            S[t, i] = f * (3.0 * b[i] - tr)
        for i in range(3, 6):
            S[t, i] = (3.0 * f) * b[i]
        JB[t] = factor * JB[t]
        VM[t] = weight
        return 0

    lax.fori_loop(0, X, stage_two, 0)
    total = jnp.sum(VM[D:D + lx, 0:ly, 0:lz])
    row8 = lax.broadcasted_iota(jnp.int32, stat.shape, 0)
    stat[...] = jnp.where(row8 == 0, top, total)

    def stage_load(t, _):
        f = gather_forces([S[t - 1, i] for i in range(6)], [S[t, i] for i in range(6)])
        k = K16[t - 1] + K16[t]
        k = k + down(k, 0)
        k = k + down(k, 1)
        dm = jnp.where(RHO[t] > 0.0, damping / ((16.0 * diag_factor) * k + shift_term), 0.0)
        DM[t] = dm
        for c in range(3):
            LOAD[t, c] = f[c]
            A[t, c] = dm * f[c]
        return 0

    lax.fori_loop(1, X, stage_load, 0)

    for sweep in range(1, ITERS):
        def stress(t, _):
            k = K16[t]
            v = cmul(raw_strain([A[t, c] for c in range(3)], [A[t + 1, c] for c in range(3)]))
            for i in range(6):
                S[t, i] = k * v[i]
            return 0

        def update(t, _):
            f = gather_forces([S[t - 1, i] for i in range(6)], [S[t, i] for i in range(6)])
            dm = DM[t]
            for c in range(3):
                a = A[t, c]
                A[t, c] = a + dm * (LOAD[t, c] - (f[c] + shift_term * a))
            return 0

        lax.fori_loop(sweep, X - sweep, stress, 0)
        lax.fori_loop(sweep + 1, X - sweep, update, 0)

    for x in range(lx):
        for c in range(3):
            adj_out[c, x] = A[D + x, c, 0:ly, 0:lz]

    y = lax.broadcasted_iota(jnp.int32, (rows, lanes), 0)
    z = lax.broadcasted_iota(jnp.int32, (rows, lanes), 1)
    y = place[1] * ly + jnp.where(y < ly + D, y, y - rows)
    z = place[2] * lz + jnp.where(z < lz + lz // 2, z, z - lanes)
    flat = jnp.where((y >= 0) & (y < ny) & (z >= 0) & (z < nz), 1.0, 0.0)

    def planar(v):
        a1, b1 = up(v, 1), down(v, 1)
        sz = a1 + b1
        sz2 = up(a1, 1) + down(b1, 1)
        vu, vd = up(v, 0), down(v, 0)
        near = sz + (vu + vd)
        far = sz2 + (up(vu, 0) + down(vd, 0))
        corner = up(sz, 0) + down(sz, 0)
        return (2.5 * v + 1.5 * near + FACE * corner + 0.5 * far, 1.5 * v + FACE * near + DIAGONAL * corner, 0.5 * v)

    h0, h1, h2 = planar(flat)

    def inside(i):
        i = place[0] * lx + i
        return jnp.where((i >= 0) & (i < nx), 1.0, 0.0)

    def stage_raw(t, _):
        rho = RHO[t]
        e = raw_strain([A[t, c] for c in range(3)], [A[t + 1, c] for c in range(3)])
        worked = sum(B[t, i] * e[i] for i in range(6))
        raw = JB[t] - (2.97 * 0.25) * (rho * rho) * worked
        i = t - D
        h = h0 * inside(i) + h1 * (inside(i - 1) + inside(i + 1)) + h2 * (inside(i - 2) + inside(i + 2))
        q = planar(jnp.where(rho > 0.0, raw / h, 0.0))
        for j in range(3):
            Q[t - (D - 2), j] = q[j][0:ly, 0:lz]
        return 0

    lax.fori_loop(D - 2, D + lx + 2, stage_raw, 0)
    for x in range(lx):
        sens_out[x] = (Q[x, 2] + Q[x + 1, 1]) + Q[x + 2, 0] + (Q[x + 3, 1] + Q[x + 4, 2])


def on_device(displacement, density):
    lx, ly, lz = density.shape
    axes = ("gx", "gy", "gz")
    counts = [lax.axis_size(a) for a in axes]
    elements = lx * ly * lz * counts[0] * counts[1] * counts[2]
    group = lx + 2
    layers = 3 * group + 3
    vmem = pl.BlockSpec(memory_space=pltpu.VMEM)
    ext = pl.pallas_call(
        gather_kernel,
        out_shape=jax.ShapeDtypeStruct((layers, 4, 2 * ly + D, lz), jnp.float32),
        in_specs=[vmem, vmem],
        out_specs=vmem,
        scratch_shapes=[
            pltpu.VMEM((2, 4, ly, lz), jnp.float32),
            pltpu.SemaphoreType.DMA((2,)),
            pltpu.SemaphoreType.DMA((2,)),
            pltpu.SemaphoreType.DMA((3,)),
            pltpu.SemaphoreType.DMA((3,)),
            pltpu.SemaphoreType.DMA((2,)),
            pltpu.SemaphoreType.DMA((2,)),
        ],
        compiler_params=pltpu.CompilerParams(has_side_effects=True, vmem_limit_bytes=60 * 2**20),
    )(displacement, density)
    place = jnp.stack([lax.axis_index(a) for a in axes]
                      + [jnp.int32(n * s) for n, s in zip(counts, (lx, ly, lz))]).astype(jnp.int32)
    X, R, L = lx + 2 * D, ly + 2 * D, 2 * lz
    f32 = jnp.float32
    adjoint, sens, stat = pl.pallas_call(
        compute_kernel,
        out_shape=(
            jax.ShapeDtypeStruct((3, lx, ly, lz), f32),
            jax.ShapeDtypeStruct((lx, ly, lz), f32),
            jax.ShapeDtypeStruct((2, lz), f32),
        ),
        in_specs=[pl.BlockSpec(memory_space=pltpu.SMEM), vmem],
        out_specs=(vmem, vmem, vmem),
        scratch_shapes=[
            pltpu.VMEM((X + 1, 3, 2 * ly + D, L), f32),
            pltpu.VMEM((X, R, L), f32),
            pltpu.VMEM((X, 6, R, L), f32),
            pltpu.VMEM((X, R, L), f32),
            pltpu.VMEM((X, R, L), f32),
            pltpu.VMEM((X, 6, R, L), f32),
            pltpu.VMEM((X, 3, R, L), f32),
            pltpu.VMEM((X, R, L), f32),
            pltpu.VMEM((X, R, L), f32),
            pltpu.VMEM((X, 3, R, L), f32),
            pltpu.VMEM((lx + 4, 3, ly, lz), f32),
        ],
        compiler_params=pltpu.CompilerParams(vmem_limit_bytes=60 * 2**20),
    )(place, ext)
    tops = lax.all_gather(stat[:, 0], axes)
    top = jnp.max(tops[:, 0])
    total = jnp.sum(tops[:, 1] * jnp.exp(tops[:, 0] - top))
    aggregate = (top + jnp.log(total)) / power_scale
    scale = jnp.exp(stat[0, 0] - top) / total * float(elements)
    return aggregate, adjoint * scale, sens * scale


def solution(mesh):
    return jax.shard_map(
        on_device,
        mesh=mesh,
        in_specs=(P(None, "gx", "gy", "gz"), P("gx", "gy", "gz")),
        out_specs=(P(), P(None, "gx", "gy", "gz"), P("gx", "gy", "gz")),
        check_vma=False,
    )
```

time: 363 us -> 140 us (0.39); the launches traced: 357 us -> 138 us
  starting transfers between devices: 117 us -> 0 us
  waiting for transfers between devices: 95.1 us -> 0 us
  Pallas kernels: 0 us -> 88.8 us
  blocking collectives: 77.5 us -> 36.3 us
  other arithmetic: 45.8 us -> 5.11 us
  local copies, waits for them, and re-layouts: 16.5 us -> 2.98 us
    ppermute x48 -> x0, starting transfers between devices: 117 us -> none  [the longest x18 55.8 us: extended(): before = lax.ppermute(last, axis, up)]
    ppermute x48 -> x0, waiting for transfers between devices: 95.1 us -> none  [the longest x18 60.5 us: extended(): after = lax.ppermute(leading, axis, down)]
    pallas_call x0 -> x2, Pallas kernels: none -> 88.8 us  [the longest x1 48.8 us: on_device(): pl.pallas_call(gather_kernel, out_shape=jax.ShapeDtypeStruct((layers, 4,...]
    psum x1 -> x0, blocking collectives: 40.4 us -> none  [on_device(): total = lax.psum(jnp.sum(jnp.exp(score - top)), ('gx', 'gy', 'gz'))]
    pmax x1 -> x0, blocking collectives: 37 us -> none  [on_device(): top = lax.pmax(local_top, ('gx', 'gy', 'gz'))]
    unnamed x0 -> x1, blocking collectives: none -> 36.3 us
    slice x33 -> x2, local copies, waits for them, and re-layouts: 13.2 us -> 1.98 us  [the longest x1 1.18 us: on_device(): scale = jnp.exp(stat[0, 0] - top) / total * float(elements)]
    mul x21 -> x2, other arithmetic: 13 us -> 3.1 us  [on_device(): return (aggregate, adjoint * scale, sens * scale)]
  transfers between devices with their start and end apart: 48 -> 0, of which waited for: 30 -> 0; matrix products, arithmetic and copies ran while one was open for 2% -> 0% of each run, Pallas kernels for 0% -> 0%
where the time goes in v1:
time: 140 us; the launch traced here: 138 us
  Pallas kernels  88.8 us (63%)
  blocking collectives  36.3 us (26%)
  between operations  5.16 us (4%)
  other arithmetic  5.11 us (4%)
  local copies, waits for them, and re-layouts  2.98 us (2%)
    pallas_call x1, Pallas kernels, on_device(): pl.pallas_call(gather_kernel, out_shape=jax.ShapeDtypeStruct((layers, 4,...  48.8 us
    pallas_call x1, Pallas kernels, on_device(): pl.pallas_call(compute_kernel, out_shape=(jax.ShapeDtypeStruct((3, lx, ly...  40 us
    unnamed x1, blocking collectives  36.3 us
    mul x2, other arithmetic, on_device(): return (aggregate, adjoint * scale, sens * scale)  3.1 us

profile of v1, /device:TPU:1, one launch (start us, length us, event | category | flops | bytes accessed | tf_op | source)
XLA Modules:
  0.0 138.4 jit_solution(2682200738289663601)
XLA Ops:
  0.6 0.7 stack.15.place
  1.3 48.8 %shard_map.49.ext = f32[33,4,40,128]{3,2,1,0:T(8,128)} custom-call(f32[3,8,16,128]{3,2,1,0:T(8,128)} %u_ref.1, f32[8,16,128]{2,1,0:T(8,128)} %rho_ref.1), custom_call_target="tpu_custom_call" | custom-call | tf_op jit(solution)/shard_map/pallas_call | solution.py:279
  50.1 40.0 %shard_map.50 = (f32[3,8,16,128]{3,2,1,0:T(8,128)}, f32[8,16,128]{2,1,0:T(8,128)}, f32[2,128]{1,0:T(2,128)}) custom-call(s32[6]{0:T(128)} %stack.15.place, f32[33,4,40,128]{3,2,1,0:T(8,128)} %shard_map.49.ext), custom_call_target="tpu_custom_call" | custom-call | tf_op jit(solution)/shard_map/pallas_call | solution.py:299
  90.1 0.8 slice_reduce_fusion.1
  90.9 0.2 dynamic-update-slice
  91.2 36.3 %all-reduce = f32[64]{0:T(128)S(1)} all-reduce(f32[64]{0:T(128)S(1)} %dynamic-update-slice), channel_id=2, replica_groups=mesh['gx'=4,'gy'=2,'gz'=4] {'gx','gy','gz'}, use_global_device_ids=true, to_apply=%add | all-reduce | flops 64 | bytes 512
  127.5 0.1 reshape.10
  127.6 0.6 slice_reduce_fusion
  128.2 1.4 %fusion = f32[]{:T(128)} fusion(f32[32,2]{1,0:T(8,128)S(1)} %reshape.10, f32[]{:T(128)} %slice_reduce_fusion), kind=kLoop, calls=%fused_computation.3 | loop fusion | flops 95 | bytes 264 | tf_op jit(solution)/shard_map/reduce_sum | solution.py:325
  129.6 1.2 slice.16
  132.8 1.5 %broadcast_multiply_fusion.1 = f32[8,16,128]{2,1,0:T(8,128)} fusion(f32[8,16,128]{2,1,0:T(8,128)} %get-tuple-element.8, f32[]{:T(128)S(6)} %mul.20), kind=kLoop, calls=%fused_computation.1 | loop fusion | flops 16384 | bytes 131076 | tf_op jit(solution)/shard_map/mul | solution.py:328
  134.2 1.6 %broadcast_multiply_fusion = f32[3,8,16,128]{3,2,1,0:T(8,128)} fusion(f32[3,8,16,128]{3,2,1,0:T(8,128)} %get-tuple-element.7, f32[]{:T(128)S(6)} %mul.20), kind=kLoop, calls=%fused_computation | loop fusion | flops 49152 | bytes 393220 | tf_op jit(solution)/shard_map/mul | solution.py:328
  (2 shorter events, 0.0 us)

commit v2 on v1

v2 whole, which is shorter than its diff:
```python
import functools
import math

import jax
import jax.numpy as jnp
from jax import lax
from jax.experimental import pallas as pl
from jax.experimental.pallas import tpu as pltpu
from jax.sharding import PartitionSpec as P

ITERS = 6
lame = 0.3 / (1.3 * 0.4)
shear = 1.0 / 2.6
power_scale = 3.0
damping = 0.6
shift_term = 0.1
diag_factor = (lame + 3.0 * shear) / 16.0
FACE = 2.5 - math.sqrt(2.0)
DIAGONAL = 2.5 - math.sqrt(3.0)
MESH = pl.DeviceIdType.MESH
D = 8
C = 16


class Message:
    def __init__(self, sems, number, axis, step, src, dst, cond=None):
        index, count = lax.axis_index(axis), lax.axis_size(axis)
        self.args = (src, dst, sems[0].at[number], sems[1].at[number], axis, index, step)
        self.sends = (index + step >= 0) & (index + step < count)
        self.gets = (index - step >= 0) & (index - step < count)
        if cond is not None:
            self.sends, self.gets = self.sends & cond, self.gets & cond
        self.dst = dst

    def copy(self, sign):
        src, dst, ssem, rsem, axis, index, step = self.args
        return pltpu.make_async_remote_copy(
            src_ref=src, dst_ref=dst, send_sem=ssem, recv_sem=rsem,
            device_id={axis: index + sign * step}, device_id_type=MESH)

    def start(self):
        pl.when(self.sends)(lambda: self.copy(1).start())

    def clear(self):
        def zero():
            self.dst[...] = jnp.zeros(self.dst.shape, jnp.float32)

        pl.when(jnp.logical_not(self.gets))(zero)

    def arrive(self):
        pl.when(self.gets)(lambda: self.copy(-1).wait_recv())

    def drain(self):
        pl.when(self.sends)(lambda: self.copy(1).wait_send())


def gather(u_ref, rho_ref, ext, T, W, V, pack, ssem, rsem):
    lx, ly, lz = rho_ref.shape
    group = lx + 2
    iy, ny = lax.axis_index("gy"), lax.axis_size("gy")
    has_above, has_below = iy + 1 < ny, iy > 0
    own, upper, lower = pl.ds(0, ly), pl.ds(ly, D), pl.ds(ly + D, D)
    u3, r1, both = pl.ds(0, 3), pl.ds(3, 1), pl.ds(0, 2)
    numbers = iter(range(64))

    def msg(axis, step, src, dst, cond=None):
        return Message((ssem, rsem), next(numbers), axis, step, src, dst, cond)

    def body(g):
        return pl.ds(g * group + 2, lx)

    def whole(g):
        return pl.ds(g * group, group)

    def halo(g):
        return pl.ds(g * group, 2)

    z = [msg("gz", -1, pack.at[0], ext.at[:, 0, own]), msg("gz", 1, pack.at[1], ext.at[:, 1, own])]
    y, x = [], []
    for step, rows, to in ((1, pl.ds(ly - D, D), lower), (-1, pl.ds(0, D), upper)):
        y.append(msg("gy", step, u_ref.at[:, :, rows], ext.at[u3, body(0), to]))
        y.append(msg("gy", step, rho_ref.at[:, rows], ext.at[3, body(0), to]))
    for step, g in ((1, 1), (-1, 2)):
        x.append(msg("gx", step, u_ref, ext.at[u3, body(g), own]))
        x.append(msg("gx", step, rho_ref, ext.at[3, body(g), own]))
    y2, x2, x3 = [], [], []
    for step, rows, to in ((1, pl.ds(ly - D, D), lower), (-1, pl.ds(0, D), upper)):
        y2.append(msg("gy", step, ext.at[:, both, rows], ext.at[:, both, to]))
    y2.append(msg("gy", -1, V, T.at[0]))
    for step, g in ((1, 1), (-1, 2)):
        x2.append(msg("gx", step, ext.at[:, halo(0), own], ext.at[:, halo(g), own]))
        x3.append(msg("gx", step, ext.at[:, whole(0), upper], ext.at[:, whole(g), upper], has_above))
        x3.append(msg("gx", step, ext.at[:, whole(0), lower], ext.at[:, whole(g), lower], has_below))
        x3.append(msg("gx", step, T.at[0], T.at[g], has_above))
    x3.append(msg("gx", -2, T.at[0], T.at[3], has_above))
    x3.append(msg("gx", -2, W.at[0], W.at[1]))
    every = z + y + x + y2 + x2 + x3

    for m in y + x:
        m.start()
    lane = lax.broadcasted_iota(jnp.int32, (ly, lz), 1)
    for c in range(4):
        first = jnp.zeros((ly, lz), jnp.float32)
        last = first
        for i in range(lx):
            tile = u_ref[c, i] if c < 3 else rho_ref[i]
            here = (lane >= C * i) & (lane < C * i + C)
            first = jnp.where(here, pltpu.roll(tile, C * i, 1) if i else tile, first)
            last = jnp.where(here, pltpu.roll(tile, (C * i + C) % lz, 1), last)
        pack[0, c] = first
        pack[1, c] = last
    for m in z:
        m.start()
    for m in every:
        m.clear()
    V[...] = jnp.zeros(V.shape, jnp.float32)
    for c in range(3):
        for i in range(lx):
            k = c * group + 2 + i
            V[k:k + 1] = u_ref[c, i, D:D + 1]
            ext[c, 2 + i, 0:ly] = u_ref[c, i]
    for i in range(lx):
        ext[3, 2 + i, 0:ly] = rho_ref[i]
    for m in z:
        m.arrive()
    for m in x2:
        m.start()
    for m in y2[:2]:
        m.start()
    for c in range(3):
        for i in range(2):
            k = c * group + i
            V[k:k + 1] = ext[c, i, D:D + 1]
    y2[2].start()
    for m in y + y2:
        m.arrive()
    for m in x3[:-1]:
        m.start()
    wide = lax.broadcasted_iota(jnp.int32, (ly + 2 * D, lz), 1)
    side = jnp.zeros((ly + 2 * D, lz), jnp.float32)
    for c in range(3):
        W[0, c] = ext[c, 2]
        for i in range(2):
            at = 2 * C * c + C * i
            tile = ext[c, i]
            tile = pltpu.roll(tile, at, 1) if at else tile
            side = jnp.where((wide >= at) & (wide < at + C), tile, side)
    W[0, 3] = side
    x3[-1].start()
    for m in x + x2 + x3:
        m.arrive()
    return every


def up(v, axis):
    return pltpu.roll(v, v.shape[axis] - 1, axis)


def down(v, axis):
    return pltpu.roll(v, 1, axis)


def raw_strain(low, high):
    g = []
    for c in range(3):
        s = low[c] + high[c]
        d = high[c] - low[c]
        s1, d1 = up(s, 1), up(d, 1)
        za, zd, xd = s + s1, s1 - s, d + d1
        g.append((xd + up(xd, 0), up(za, 0) - za, zd + up(zd, 0)))
    return (g[0][0], g[1][1], g[2][2], g[1][0] + g[0][1], g[2][1] + g[1][2], g[0][2] + g[2][0])


def cmul(t):
    tr = lame * (t[0] + t[1] + t[2])
    return [tr + (2.0 * shear) * t[i] for i in range(3)] + [shear * t[i] for i in range(3, 6)]


ROWS = ((0, 3, 5), (3, 1, 4), (5, 4, 2))


def gather_forces(a, b):
    out = []
    for c in range(3):
        i, j, k = ROWS[c]
        x = a[i] - b[i]
        y = a[j] + b[j]
        z = a[k] + b[k]
        w = down(x + y, 0) + (x - y)
        v = down(z, 0) + z
        out.append(down(w + v, 1) + (w - v))
    return out


def kernel(u_ref, rho_ref, agg_out, adj_out, sens_out, ext, T, W, V, pack, ssem, rsem, ST, gsem, hsem, U, RHO, B, VM, JB, S, LOAD, DM, K16, A, Q):
    lx, ly, lz = sens_out.shape
    axes = ("gx", "gy", "gz")
    place = [lax.axis_index(a) for a in axes]
    counts = [lax.axis_size(a) for a in axes]
    nx, ny, nz = counts[0] * lx, counts[1] * ly, counts[2] * lz
    devices = counts[0] * counts[1] * counts[2]
    me = (place[0] * counts[1] + place[1]) * counts[2] + place[2]
    group = lx + 2
    pending = gather(u_ref, rho_ref, ext, T, W, V, pack, ssem, rsem)
    X = lx + 2 * D
    rows, lanes = ly + 2 * D, 2 * lz
    wide = (ly + 3 * D, lz)
    lane = lax.broadcasted_iota(jnp.int32, wide, 1)

    def tall(v, row):
        return jnp.concatenate([v[0:ly + D], jnp.broadcast_to(row, (D, lz)), v[ly + D:rows]], axis=0)

    def turn(v, amount):
        return pltpu.roll(v, amount % lz, 1) if amount % lz else v

    for t in range(X + 1):
        g, xi = divmod(t, lx)
        base = (group, 0, 2 * group, 0)[g]
        tg = (1, 0, 2, 3)[g]
        for c in range(3):
            k = c * group
            if t < X:
                main, above, below = ext[c, base + 2 + xi], ext[c, base], ext[c, base + 1]
                above, below = turn(above, -C * xi), turn(below, -C - C * xi)
            else:
                main, side = W[1, c], W[1, 3]
                above, below = turn(side, -2 * C * c), turn(side, -2 * C * c - 2 * C)
            above = tall(above, turn(T[tg, k:k + 1], -C * xi))
            below = tall(below, turn(T[tg, k + 1:k + 2], -C - C * xi))
            U[t, c, :, 0:lz] = tall(main, T[tg, k + 2 + xi:k + 3 + xi])
            U[t, c, :, lz:lanes] = jnp.where(lane < D + 1, above, jnp.where(lane >= lz - D, below, 0.0))
        if t < X:
            above, below = turn(ext[3, base], -C * xi), turn(ext[3, base + 1], -C - C * xi)
            thin = lane[0:rows]
            RHO[t, :, 0:lz] = ext[3, base + 2 + xi]
            RHO[t, :, lz:lanes] = jnp.where(thin < D, above, jnp.where(thin >= lz - D, below, 0.0))

    def cut(v):
        return jnp.concatenate([v[0:ly + D], v[ly + 2 * D:ly + 3 * D]], axis=0)

    def stage_one(t, best):
        low = [U[t, c] for c in range(3)]
        high = [U[t + 1, c] for c in range(3)]
        b = cmul([cut(0.25 * e) for e in raw_strain(low, high)])
        j = (b[0] * b[0] + b[1] * b[1] + b[2] * b[2] - b[0] * b[1] - b[1] * b[2] - b[2] * b[0]
             + 3.0 * (b[3] * b[3] + b[4] * b[4] + b[5] * b[5]))
        rho = RHO[t]
        vm = jnp.sqrt(rho * j + 1.0)
        for i in range(6):
            B[t, i] = b[i]
        JB[t] = j
        VM[t] = vm
        K16[t] = jnp.where(rho > 0.0, (0.01 + 0.99 * (rho * rho * rho)) * 0.0625, 0.0)
        return jnp.maximum(best, vm)

    best = lax.fori_loop(0, X, stage_one, jnp.ones((rows, lanes), jnp.float32))
    top = power_scale * jnp.max(best)

    def stage_two(t, _):
        vm = VM[t]
        weight = jnp.exp(power_scale * vm - top)
        factor = weight / (2.0 * vm)
        f = factor * RHO[t] * (0.5 * shear)
        b = [B[t, i] for i in range(6)]
        tr = b[0] + b[1] + b[2]
        for i in range(3):
            S[t, i] = f * (3.0 * b[i] - tr)
        for i in range(3, 6):
            S[t, i] = (3.0 * f) * b[i]
        JB[t] = factor * JB[t]
        VM[t] = weight
        return 0

    lax.fori_loop(0, X, stage_two, 0)
    total = jnp.sum(VM[D:D + lx, 0:ly, 0:lz])
    row8 = lax.broadcasted_iota(jnp.int32, (8, lz), 0)
    ST[me] = jnp.where(row8 == 0, top, total)

    def partner(k, sign):
        other = (me + sign * k + devices) % devices
        there = (other // (counts[1] * counts[2]), (other // counts[2]) % counts[1], other % counts[2])
        slot = me if sign > 0 else other
        return pltpu.make_async_remote_copy(
            src_ref=ST.at[slot], dst_ref=ST.at[slot], send_sem=gsem.at[k], recv_sem=hsem.at[k],
            device_id=there, device_id_type=MESH)

    def give(k, _):
        partner(k, 1).start()
        return 0

    lax.fori_loop(1, devices, give, 0)

    def stage_load(t, _):
        f = gather_forces([S[t - 1, i] for i in range(6)], [S[t, i] for i in range(6)])
        k = K16[t - 1] + K16[t]
        k = k + down(k, 0)
        k = k + down(k, 1)
        dm = jnp.where(RHO[t] > 0.0, damping / ((16.0 * diag_factor) * k + shift_term), 0.0)
        DM[t] = dm
        for c in range(3):
            LOAD[t, c] = f[c]
            A[t, c] = dm * f[c]
        return 0

    lax.fori_loop(1, X, stage_load, 0)

    for sweep in range(1, ITERS):
        def stress(t, _):
            k = K16[t]
            v = cmul(raw_strain([A[t, c] for c in range(3)], [A[t + 1, c] for c in range(3)]))
            for i in range(6):
                S[t, i] = k * v[i]
            return 0

        def update(t, _):
            f = gather_forces([S[t - 1, i] for i in range(6)], [S[t, i] for i in range(6)])
            dm = DM[t]
            for c in range(3):
                a = A[t, c]
                A[t, c] = a + dm * (LOAD[t, c] - (f[c] + shift_term * a))
            return 0

        lax.fori_loop(sweep, X - sweep, stress, 0)
        lax.fori_loop(sweep + 1, X - sweep, update, 0)

    y = lax.broadcasted_iota(jnp.int32, (rows, lanes), 0)
    z = lax.broadcasted_iota(jnp.int32, (rows, lanes), 1)
    y = place[1] * ly + jnp.where(y < ly + D, y, y - rows)
    z = place[2] * lz + jnp.where(z < lz + lz // 2, z, z - lanes)
    flat = jnp.where((y >= 0) & (y < ny) & (z >= 0) & (z < nz), 1.0, 0.0)

    def planar(v):
        a1, b1 = up(v, 1), down(v, 1)
        sz = a1 + b1
        sz2 = up(a1, 1) + down(b1, 1)
        vu, vd = up(v, 0), down(v, 0)
        near = sz + (vu + vd)
        far = sz2 + (up(vu, 0) + down(vd, 0))
        corner = up(sz, 0) + down(sz, 0)
        return (2.5 * v + 1.5 * near + FACE * corner + 0.5 * far, 1.5 * v + FACE * near + DIAGONAL * corner, 0.5 * v)

    h0, h1, h2 = planar(flat)

    def inside(i):
        i = place[0] * lx + i
        return jnp.where((i >= 0) & (i < nx), 1.0, 0.0)

    def stage_raw(t, _):
        rho = RHO[t]
        e = raw_strain([A[t, c] for c in range(3)], [A[t + 1, c] for c in range(3)])
        worked = sum(B[t, i] * e[i] for i in range(6))
        raw = JB[t] - (2.97 * 0.25) * (rho * rho) * worked
        i = t - D
        h = h0 * inside(i) + h1 * (inside(i - 1) + inside(i + 1)) + h2 * (inside(i - 2) + inside(i + 2))
        q = planar(jnp.where(rho > 0.0, raw / h, 0.0))
        for j in range(3):
            Q[t - (D - 2), j] = q[j][0:ly, 0:lz]
        return 0

    lax.fori_loop(D - 2, D + lx + 2, stage_raw, 0)

    def take(k, _):
        partner(k, -1).wait_recv()
        partner(k, 1).wait_send()
        return 0

    lax.fori_loop(1, devices, take, 0)
    for m in pending:
        m.drain()
    tops, totals = ST[:, 0, :], ST[:, 1, :]
    peak = jnp.max(tops, axis=0, keepdims=True)
    sums = jnp.sum(totals * jnp.exp(tops - peak), axis=0, keepdims=True)
    agg_out[0, 0] = jnp.max((peak + jnp.log(sums)) / power_scale)
    scale = jnp.exp(top - peak) / sums * float(nx * ny * nz)
    for x in range(lx):
        for c in range(3):
            adj_out[c, x] = A[D + x, c, 0:ly, 0:lz] * scale
        sens_out[x] = ((Q[x, 2] + Q[x + 1, 1]) + Q[x + 2, 0] + (Q[x + 3, 1] + Q[x + 4, 2])) * scale


def on_device(displacement, density):
    lx, ly, lz = density.shape
    devices = lax.axis_size("gx") * lax.axis_size("gy") * lax.axis_size("gz")
    group = lx + 2
    vmem = pl.BlockSpec(memory_space=pltpu.VMEM)
    X, R, L = lx + 2 * D, ly + 2 * D, 2 * lz
    f32 = jnp.float32
    shapes = [
        (X + 1, 3, ly + 3 * D, L), (X, R, L), (X, 6, R, L), (X, R, L), (X, R, L), (X, 6, R, L),
        (X, 3, R, L), (X, R, L), (X, R, L), (X, 3, R, L), (lx + 4, 3, ly, lz),
    ]
    dma = pltpu.SemaphoreType.DMA
    aggregate, adjoint, sens = pl.pallas_call(
        kernel,
        out_shape=(
            jax.ShapeDtypeStruct((1, 1), f32),
            jax.ShapeDtypeStruct((3, lx, ly, lz), f32),
            jax.ShapeDtypeStruct((lx, ly, lz), f32),
        ),
        in_specs=[vmem, vmem],
        out_specs=(pl.BlockSpec(memory_space=pltpu.SMEM), vmem, vmem),
        scratch_shapes=[
            pltpu.VMEM((4, 3 * group, R, lz), f32),
            pltpu.VMEM((4, 32, lz), f32),
            pltpu.VMEM((2, 4, R, lz), f32),
            pltpu.VMEM((32, lz), f32),
            pltpu.VMEM((2, 4, ly, lz), f32),
            dma((32,)), dma((32,)),
            pltpu.VMEM((devices, 8, lz), f32),
            dma((devices,)), dma((devices,)),
        ] + [pltpu.VMEM(s, f32) for s in shapes],
        compiler_params=pltpu.CompilerParams(has_side_effects=True, vmem_limit_bytes=60 * 2**20),
    )(displacement, density)
    return aggregate[0, 0], adjoint, sens


def solution(mesh):
    return jax.shard_map(
        on_device,
        mesh=mesh,
        in_specs=(P(None, "gx", "gy", "gz"), P("gx", "gy", "gz")),
        out_specs=(P(), P(None, "gx", "gy", "gz"), P("gx", "gy", "gz")),
        check_vma=False,
    )
```

time: 140 us -> 71.8 us (0.51)
  blocking collectives: 36.3 us -> 0 us
  Pallas kernels: 88.8 us -> 66.1 us
  other arithmetic: 5.11 us -> 0 us
  between operations: 5.16 us -> 2.32 us
    unnamed x1 -> x0, blocking collectives: 36.3 us -> none
    pallas_call x2 -> x1, Pallas kernels: 88.8 us -> 66.1 us  [on_device(): pl.pallas_call(kernel, out_shape=(jax.ShapeDtypeStruct((1, 1), f32), jax....]
    mul x2 -> x0, other arithmetic: 3.1 us -> none  [on_device(): return (aggregate, adjoint * scale, sens * scale)]
    unnamed x2 -> x4, local copies, waits for them, and re-layouts: 0.24 us -> 2.28 us
    slice x2 -> x0, local copies, waits for them, and re-layouts: 1.98 us -> none  [the longest x1 1.18 us: on_device(): scale = jnp.exp(stat[0, 0] - top) / total * float(elements)]
where the time goes in v2:
time: 71.8 us; the launch traced here: 70.7 us
  Pallas kernels  66.1 us (92%)
  between operations  2.32 us (3%)
  local copies, waits for them, and re-layouts  2.28 us (3%)
    pallas_call x1, Pallas kernels, on_device(): pl.pallas_call(kernel, out_shape=(jax.ShapeDtypeStruct((1, 1), f32), jax....  66.1 us
    unnamed x4, local copies, waits for them, and re-layouts  2.28 us

profile of v2, /device:TPU:1, one launch (start us, length us, event | category | flops | bytes accessed | tf_op | source)
XLA Modules:
  0.0 70.7 jit_solution(8428450014646317388)
XLA Ops:
  0.6 66.1 %shard_map.49 = (f32[1,1]{1,0:T(1,128)}, f32[3,8,16,128]{3,2,1,0:T(8,128)}, f32[8,16,128]{2,1,0:T(8,128)}) custom-call(f32[3,8,16,128]{3,2,1,0:T(8,128)} %u_ref.1, f32[8,16,128]{2,1,0:T(8,128)} %rho_ref.1), custom_call_target="tpu_custom_call" | custom-call | tf_op jit(solution)/shard_map/pallas_call | solution.py:393
  67.3 0.0 copy-start
  67.3 1.6 %copy.9 = f32[3,8,16,128]{3,2,1,0:T(8,128)} copy(f32[3,8,16,128]{3,2,1,0:T(8,128)} %get-tuple-element.13) | data formatting | bytes 393216
  69.0 0.0 copy-done
  69.0 0.6 copy.10
Async XLA Ops:
  67.3 1.7 %copy-start = (f32[8,16,128]{2,1,0:T(8,128)S(1)}, f32[8,16,128]{2,1,0:T(8,128)}, u32[]{:S(2)}) copy-start(f32[8,16,128]{2,1,0:T(8,128)} %get-tuple-element.14) | copy-start | bytes 196612

commit v3 on v2

--- a/solution.py
+++ b/solution.py
@@ -147,9 +147,9 @@
             side = jnp.where((wide >= at) & (wide < at + C), tile, side)
     W[0, 3] = side
     x3[-1].start()
-    for m in x + x2 + x3:
-        m.arrive()
-    return every
+    lower_side = x[:2] + x2[:1] + x3[:3]
+    upper_side = x[2:] + x2[1:] + x3[3:6]
+    return every, (lower_side, upper_side, x3[6:])
 
 
 def up(v, axis):
@@ -195,13 +195,19 @@
 def kernel(u_ref, rho_ref, agg_out, adj_out, sens_out, ext, T, W, V, pack, ssem, rsem, ST, gsem, hsem, U, RHO, B, VM, JB, S, LOAD, DM, K16, A, Q):
     lx, ly, lz = sens_out.shape
     axes = ("gx", "gy", "gz")
+    barrier = pltpu.get_barrier_semaphore()
+    friends = 0
+    for axis in axes:
+        index, count = lax.axis_index(axis), lax.axis_size(axis)
+        friends += count - 1
+        for step in range(1, count):
+            pl.semaphore_signal(barrier, inc=1, device_id={axis: (index + step) % count}, device_id_type=MESH)
+    pl.semaphore_wait(barrier, friends)
     place = [lax.axis_index(a) for a in axes]
     counts = [lax.axis_size(a) for a in axes]
     nx, ny, nz = counts[0] * lx, counts[1] * ly, counts[2] * lz
-    devices = counts[0] * counts[1] * counts[2]
-    me = (place[0] * counts[1] + place[1]) * counts[2] + place[2]
     group = lx + 2
-    pending = gather(u_ref, rho_ref, ext, T, W, V, pack, ssem, rsem)
+    pending, arrivals = gather(u_ref, rho_ref, ext, T, W, V, pack, ssem, rsem)
     X = lx + 2 * D
     rows, lanes = ly + 2 * D, 2 * lz
     wide = (ly + 3 * D, lz)
@@ -213,7 +219,7 @@
     def turn(v, amount):
         return pltpu.roll(v, amount % lz, 1) if amount % lz else v
 
-    for t in range(X + 1):
+    def unpack(t):
         g, xi = divmod(t, lx)
         base = (group, 0, 2 * group, 0)[g]
         tg = (1, 0, 2, 3)[g]
@@ -253,7 +259,24 @@
         K16[t] = jnp.where(rho > 0.0, (0.01 + 0.99 * (rho * rho * rho)) * 0.0625, 0.0)
         return jnp.maximum(best, vm)
 
-    best = lax.fori_loop(0, X, stage_one, jnp.ones((rows, lanes), jnp.float32))
+    best = jnp.ones((rows, lanes), jnp.float32)
+    for t in range(D, D + lx):
+        unpack(t)
+    best = lax.fori_loop(D, D + lx - 1, stage_one, best)
+    for m in arrivals[0]:
+        m.arrive()
+    for t in range(D):
+        unpack(t)
+    best = lax.fori_loop(0, D, stage_one, best)
+    for m in arrivals[1]:
+        m.arrive()
+    for t in range(D + lx, X):
+        unpack(t)
+    best = lax.fori_loop(D + lx - 1, X - 1, stage_one, best)
+    for m in arrivals[2]:
+        m.arrive()
+    unpack(X)
+    best = stage_one(X - 1, best)
     top = power_scale * jnp.max(best)
 
     def stage_two(t, _):
@@ -274,21 +297,35 @@
     lax.fori_loop(0, X, stage_two, 0)
     total = jnp.sum(VM[D:D + lx, 0:ly, 0:lz])
     row8 = lax.broadcasted_iota(jnp.int32, (8, lz), 0)
-    ST[me] = jnp.where(row8 == 0, top, total)
-
-    def partner(k, sign):
-        other = (me + sign * k + devices) % devices
-        there = (other // (counts[1] * counts[2]), (other // counts[2]) % counts[1], other % counts[2])
-        slot = me if sign > 0 else other
+    starts = (0, counts[0], counts[0] + counts[1])
+    state = jnp.where(row8 == 0, top, total)
+
+    def partner(p, k, sign):
+        index, count = place[p], counts[p]
+        other = (index + sign * k) % count if sign > 0 else (index - k + count) % count
+        slot = starts[p] + (index if sign > 0 else other)
         return pltpu.make_async_remote_copy(
-            src_ref=ST.at[slot], dst_ref=ST.at[slot], send_sem=gsem.at[k], recv_sem=hsem.at[k],
-            device_id=there, device_id_type=MESH)
-
-    def give(k, _):
-        partner(k, 1).start()
-        return 0
-
-    lax.fori_loop(1, devices, give, 0)
+            src_ref=ST.at[slot], dst_ref=ST.at[slot],
+            send_sem=gsem.at[starts[p] + k], recv_sem=hsem.at[starts[p] + k],
+            device_id={axes[p]: other}, device_id_type=MESH)
+
+    def give(p, value):
+        ST[starts[p] + place[p]] = value
+        for k in range(1, counts[p]):
+            partner(p, k, 1).start()
+
+    def take(p):
+        for k in range(1, counts[p]):
+            partner(p, k, -1).wait_recv()
+        for k in range(1, counts[p]):
+            partner(p, k, 1).wait_send()
+        tiles = ST[starts[p]:starts[p] + counts[p]]
+        tops, totals = tiles[:, 0, :], tiles[:, 1, :]
+        peak = jnp.max(tops, axis=0, keepdims=True)
+        sums = jnp.sum(totals * jnp.exp(tops - peak), axis=0, keepdims=True)
+        return peak, sums
+
+    give(0, state)
 
     def stage_load(t, _):
         f = gather_forces([S[t - 1, i] for i in range(6)], [S[t, i] for i in range(6)])
@@ -322,6 +359,9 @@
 
         lax.fori_loop(sweep, X - sweep, stress, 0)
         lax.fori_loop(sweep + 1, X - sweep, update, 0)
+        if sweep <= 2:
+            peak, sums = take(sweep - 1)
+            give(sweep, jnp.where(row8 == 0, peak, sums))
 
     y = lax.broadcasted_iota(jnp.int32, (rows, lanes), 0)
     z = lax.broadcasted_iota(jnp.int32, (rows, lanes), 1)
@@ -358,18 +398,9 @@
         return 0
 
     lax.fori_loop(D - 2, D + lx + 2, stage_raw, 0)
-
-    def take(k, _):
-        partner(k, -1).wait_recv()
-        partner(k, 1).wait_send()
-        return 0
-
-    lax.fori_loop(1, devices, take, 0)
+    peak, sums = take(2)
     for m in pending:
         m.drain()
-    tops, totals = ST[:, 0, :], ST[:, 1, :]
-    peak = jnp.max(tops, axis=0, keepdims=True)
-    sums = jnp.sum(totals * jnp.exp(tops - peak), axis=0, keepdims=True)
     agg_out[0, 0] = jnp.max((peak + jnp.log(sums)) / power_scale)
     scale = jnp.exp(top - peak) / sums * float(nx * ny * nz)
     for x in range(lx):
@@ -380,7 +411,7 @@
 
 def on_device(displacement, density):
     lx, ly, lz = density.shape
-    devices = lax.axis_size("gx") * lax.axis_size("gy") * lax.axis_size("gz")
+    slots = lax.axis_size("gx") + lax.axis_size("gy") + lax.axis_size("gz")
     group = lx + 2
     vmem = pl.BlockSpec(memory_space=pltpu.VMEM)
     X, R, L = lx + 2 * D, ly + 2 * D, 2 * lz
@@ -406,10 +437,10 @@
             pltpu.VMEM((32, lz), f32),
             pltpu.VMEM((2, 4, ly, lz), f32),
             dma((32,)), dma((32,)),
-            pltpu.VMEM((devices, 8, lz), f32),
-            dma((devices,)), dma((devices,)),
+            pltpu.VMEM((slots, 8, lz), f32),
+            dma((slots,)), dma((slots,)),
         ] + [pltpu.VMEM(s, f32) for s in shapes],
-        compiler_params=pltpu.CompilerParams(has_side_effects=True, vmem_limit_bytes=60 * 2**20),
+        compiler_params=pltpu.CompilerParams(has_side_effects=True, collective_id=0, vmem_limit_bytes=60 * 2**20),
     )(displacement, density)
     return aggregate[0, 0], adjoint, sens
 

time: 71.8 us -> 59.8 us (0.83)
  Pallas kernels: 66.1 us -> 54.2 us
    pallas_call x1, Pallas kernels: 66.1 us -> 54.2 us  [on_device(): pl.pallas_call(kernel, out_shape=(jax.ShapeDtypeStruct((1, 1), f32), jax....]
where the time goes in v3:
time: 59.8 us; the launch traced here: 58.8 us
  Pallas kernels  54.2 us (91%)
  between operations  2.32 us (4%)
  local copies, waits for them, and re-layouts  2.28 us (4%)
    pallas_call x1, Pallas kernels, on_device(): pl.pallas_call(kernel, out_shape=(jax.ShapeDtypeStruct((1, 1), f32), jax....  54.2 us
    unnamed x4, local copies, waits for them, and re-layouts  2.28 us

profile of v3, /device:TPU:1, one launch (start us, length us, event | category | flops | bytes accessed | tf_op | source)
XLA Modules:
  0.0 58.8 jit_solution(17956397572048847282)
XLA Ops:
  0.6 54.2 %shard_map.49 = (f32[1,1]{1,0:T(1,128)}, f32[3,8,16,128]{3,2,1,0:T(8,128)}, f32[8,16,128]{2,1,0:T(8,128)}) custom-call(f32[3,8,16,128]{3,2,1,0:T(8,128)} %u_ref.1, f32[8,16,128]{2,1,0:T(8,128)} %rho_ref.1), custom_call_target="tpu_custom_call" | custom-call | tf_op jit(solution)/shard_map/pallas_call | solution.py:424
  55.4 0.0 copy-start
  55.4 1.6 %copy.9 = f32[3,8,16,128]{3,2,1,0:T(8,128)} copy(f32[3,8,16,128]{3,2,1,0:T(8,128)} %get-tuple-element.13) | data formatting | bytes 393216
  57.1 0.0 copy-done
  57.1 0.6 %copy.10 = f32[8,16,128]{2,1,0:T(8,128)} copy(f32[8,16,128]{2,1,0:T(8,128)S(1)} %copy-done) | data formatting | bytes 131072
Async XLA Ops:
  55.4 1.7 %copy-start = (f32[8,16,128]{2,1,0:T(8,128)S(1)}, f32[8,16,128]{2,1,0:T(8,128)}, u32[]{:S(2)}) copy-start(f32[8,16,128]{2,1,0:T(8,128)} %get-tuple-element.14) | copy-start | bytes 196612

commit v4 on v3

--- a/solution.py
+++ b/solution.py
@@ -192,7 +192,7 @@
     return out
 
 
-def kernel(u_ref, rho_ref, agg_out, adj_out, sens_out, ext, T, W, V, pack, ssem, rsem, ST, gsem, hsem, U, RHO, B, VM, JB, S, LOAD, DM, K16, A, Q):
+def kernel(u_ref, rho_ref, agg_out, adj_out, sens_out, ext, T, W, V, pack, ssem, rsem, ST, gsem, hsem, U, RHO, B, VM, JB, S, LOAD, DM, K16, A, Q, EM):
     lx, ly, lz = sens_out.shape
     axes = ("gx", "gy", "gz")
     barrier = pltpu.get_barrier_semaphore()
@@ -256,7 +256,7 @@
             B[t, i] = b[i]
         JB[t] = j
         VM[t] = vm
-        K16[t] = jnp.where(rho > 0.0, (0.01 + 0.99 * (rho * rho * rho)) * 0.0625, 0.0)
+        K16[t] = jnp.where(rho > 0.0, (0.01 + 0.99 * (rho * rho * rho)) * (0.125 * shear), 0.0)
         return jnp.maximum(best, vm)
 
     best = jnp.ones((rows, lanes), jnp.float32)
@@ -267,12 +267,12 @@
         m.arrive()
     for t in range(D):
         unpack(t)
-    best = lax.fori_loop(0, D, stage_one, best)
+    best = lax.fori_loop(0, D, stage_one, best, unroll=2)
     for m in arrivals[1]:
         m.arrive()
     for t in range(D + lx, X):
         unpack(t)
-    best = lax.fori_loop(D + lx - 1, X - 1, stage_one, best)
+    best = lax.fori_loop(D + lx - 1, X - 1, stage_one, best, unroll=2)
     for m in arrivals[2]:
         m.arrive()
     unpack(X)
@@ -294,7 +294,7 @@
         VM[t] = weight
         return 0
 
-    lax.fori_loop(0, X, stage_two, 0)
+    lax.fori_loop(0, X, stage_two, 0, unroll=2)
     total = jnp.sum(VM[D:D + lx, 0:ly, 0:lz])
     row8 = lax.broadcasted_iota(jnp.int32, (8, lz), 0)
     starts = (0, counts[0], counts[0] + counts[1])
@@ -332,33 +332,38 @@
         k = K16[t - 1] + K16[t]
         k = k + down(k, 0)
         k = k + down(k, 1)
-        dm = jnp.where(RHO[t] > 0.0, damping / ((16.0 * diag_factor) * k + shift_term), 0.0)
+        dm = jnp.where(RHO[t] > 0.0, damping / ((8.0 * diag_factor / shear) * k + shift_term), 0.0)
         DM[t] = dm
+        EM[t] = 1.0 - shift_term * dm
         for c in range(3):
-            LOAD[t, c] = f[c]
+            LOAD[t, c] = dm * f[c]
             A[t, c] = dm * f[c]
         return 0
 
-    lax.fori_loop(1, X, stage_load, 0)
+    stage_load(1, 0)
+    lax.fori_loop(2, X, stage_load, 0, unroll=2)
 
     for sweep in range(1, ITERS):
         def stress(t, _):
+            n = raw_strain([A[t, c] for c in range(3)], [A[t + 1, c] for c in range(3)])
             k = K16[t]
-            v = cmul(raw_strain([A[t, c] for c in range(3)], [A[t + 1, c] for c in range(3)]))
-            for i in range(6):
-                S[t, i] = k * v[i]
+            half = 0.5 * k
+            tr = (lame / (2.0 * shear)) * (n[0] + n[1] + n[2])
+            for i in range(3):
+                S[t, i] = k * (n[i] + tr)
+            for i in range(3, 6):
+                S[t, i] = half * n[i]
             return 0
 
         def update(t, _):
             f = gather_forces([S[t - 1, i] for i in range(6)], [S[t, i] for i in range(6)])
-            dm = DM[t]
+            dm, keep = DM[t], EM[t]
             for c in range(3):
-                a = A[t, c]
-                A[t, c] = a + dm * (LOAD[t, c] - (f[c] + shift_term * a))
+                A[t, c] = (keep * A[t, c] + LOAD[t, c]) - dm * f[c]
             return 0
 
-        lax.fori_loop(sweep, X - sweep, stress, 0)
-        lax.fori_loop(sweep + 1, X - sweep, update, 0)
+        lax.fori_loop(sweep, X - sweep, stress, 0, unroll=2)
+        lax.fori_loop(sweep + 1, X - sweep + 1, update, 0, unroll=2)
         if sweep <= 2:
             peak, sums = take(sweep - 1)
             give(sweep, jnp.where(row8 == 0, peak, sums))
@@ -369,14 +374,17 @@
     z = place[2] * lz + jnp.where(z < lz + lz // 2, z, z - lanes)
     flat = jnp.where((y >= 0) & (y < ny) & (z >= 0) & (z < nz), 1.0, 0.0)
 
-    def planar(v):
+    def planar(v, tall=None, wide=None):
+        own = (slice(0, tall), slice(0, wide))
         a1, b1 = up(v, 1), down(v, 1)
-        sz = a1 + b1
-        sz2 = up(a1, 1) + down(b1, 1)
-        vu, vd = up(v, 0), down(v, 0)
-        near = sz + (vu + vd)
-        far = sz2 + (up(vu, 0) + down(vd, 0))
-        corner = up(sz, 0) + down(sz, 0)
+        sz = (a1 + b1)[:, 0:wide]
+        sz2 = up(a1, 1)[own] + down(b1, 1)[own]
+        n = v[:, 0:wide]
+        vu, vd = up(n, 0), down(n, 0)
+        near = sz[0:tall] + (vu + vd)[0:tall]
+        far = sz2 + (up(vu, 0) + down(vd, 0))[0:tall]
+        corner = (up(sz, 0) + down(sz, 0))[0:tall]
+        v = v[own]
         return (2.5 * v + 1.5 * near + FACE * corner + 0.5 * far, 1.5 * v + FACE * near + DIAGONAL * corner, 0.5 * v)
 
     h0, h1, h2 = planar(flat)
@@ -392,12 +400,12 @@
         raw = JB[t] - (2.97 * 0.25) * (rho * rho) * worked
         i = t - D
         h = h0 * inside(i) + h1 * (inside(i - 1) + inside(i + 1)) + h2 * (inside(i - 2) + inside(i + 2))
-        q = planar(jnp.where(rho > 0.0, raw / h, 0.0))
+        q = planar(jnp.where(rho > 0.0, raw / h, 0.0), ly, lz)
         for j in range(3):
-            Q[t - (D - 2), j] = q[j][0:ly, 0:lz]
+            Q[t - (D - 2), j] = q[j]
         return 0
 
-    lax.fori_loop(D - 2, D + lx + 2, stage_raw, 0)
+    lax.fori_loop(D - 2, D + lx + 2, stage_raw, 0, unroll=2)
     peak, sums = take(2)
     for m in pending:
         m.drain()
@@ -418,7 +426,7 @@
     f32 = jnp.float32
     shapes = [
         (X + 1, 3, ly + 3 * D, L), (X, R, L), (X, 6, R, L), (X, R, L), (X, R, L), (X, 6, R, L),
-        (X, 3, R, L), (X, R, L), (X, R, L), (X, 3, R, L), (lx + 4, 3, ly, lz),
+        (X, 3, R, L), (X, R, L), (X, R, L), (X, 3, R, L), (lx + 4, 3, ly, lz), (X, R, L),
     ]
     dma = pltpu.SemaphoreType.DMA
     aggregate, adjoint, sens = pl.pallas_call(

time: 59.8 us -> 50.5 us (0.84)
  Pallas kernels: 54.2 us -> 44.9 us
    pallas_call x1, Pallas kernels: 54.2 us -> 44.9 us  [on_device(): pl.pallas_call(kernel, out_shape=(jax.ShapeDtypeStruct((1, 1), f32), jax....]
where the time goes in v4:
time: 50.5 us; the launch traced here: 49.5 us
  Pallas kernels  44.9 us (89%)
  between operations  2.32 us (5%)
  local copies, waits for them, and re-layouts  2.28 us (5%)
    pallas_call x1, Pallas kernels, on_device(): pl.pallas_call(kernel, out_shape=(jax.ShapeDtypeStruct((1, 1), f32), jax....  44.9 us
    unnamed x4, local copies, waits for them, and re-layouts  2.28 us

profile of v4, /device:TPU:1, one launch (start us, length us, event | category | flops | bytes accessed | tf_op | source)
XLA Modules:
  0.0 49.5 jit_solution(12751650537554891222)
XLA Ops:
  0.6 44.9 %shard_map.49 = (f32[1,1]{1,0:T(1,128)}, f32[3,8,16,128]{3,2,1,0:T(8,128)}, f32[8,16,128]{2,1,0:T(8,128)}) custom-call(f32[3,8,16,128]{3,2,1,0:T(8,128)} %u_ref.1, f32[8,16,128]{2,1,0:T(8,128)} %rho_ref.1), custom_call_target="tpu_custom_call" | custom-call | tf_op jit(solution)/shard_map/pallas_call | solution.py:432
  46.1 0.0 copy-start
  46.1 1.6 %copy.9 = f32[3,8,16,128]{3,2,1,0:T(8,128)} copy(f32[3,8,16,128]{3,2,1,0:T(8,128)} %get-tuple-element.13) | data formatting | bytes 393216
  47.8 0.0 copy-done
  47.8 0.6 %copy.10 = f32[8,16,128]{2,1,0:T(8,128)} copy(f32[8,16,128]{2,1,0:T(8,128)S(1)} %copy-done) | data formatting | bytes 131072
Async XLA Ops:
  46.1 1.7 %copy-start = (f32[8,16,128]{2,1,0:T(8,128)S(1)}, f32[8,16,128]{2,1,0:T(8,128)}, u32[]{:S(2)}) copy-start(f32[8,16,128]{2,1,0:T(8,128)} %get-tuple-element.14) | copy-start | bytes 196612
